TPU v7x, 32 devices: a whole 2x2x4 slice. The times are simulated.
32 devices in a mesh: fsdp: 32 (over z, y, x, core).
Axes of the slice: x: 2, y: 2, z: 4, core: 2. Of those that a mesh axis runs over, the one named last changes fastest.
Arguments:
- tokens: int32 [32, 512], P('fsdp')
- positions: int32 [32, 512], P('fsdp')
- embed_table: bfloat16 [49152, 960], P('fsdp')
- attn_norm: bfloat16 [960], P('fsdp')
- w_query: bfloat16 [960, 960], P('fsdp')
- w_key: bfloat16 [960, 320], P('fsdp')
- w_value: bfloat16 [960, 320], P('fsdp')
- q_norm: bfloat16 [64], replicated
- k_norm: bfloat16 [64], replicated
- w_out: bfloat16 [960, 960], P('fsdp')
- mlp_norm: bfloat16 [960], P('fsdp')
- w_gate: bfloat16 [960, 2560], P('fsdp')
- w_up: bfloat16 [960, 2560], P('fsdp')
- w_down: bfloat16 [2560, 960], P('fsdp')
- dy_out: bfloat16 [32, 512, 960], P('fsdp')
Outputs:
- output 1: bfloat16 [32, 512, 960], P('fsdp')
- output 2: float32 [49152, 960], P('fsdp')
- output 3: float32 [960], P('fsdp')
- output 4: float32 [960, 960], P('fsdp')
- output 5: float32 [960, 320], P('fsdp')
- output 6: float32 [960, 320], P('fsdp')
- output 7: float32 [64], replicated
- output 8: float32 [64], replicated
- output 9: float32 [960, 960], P('fsdp')
- output 10: float32 [960], P('fsdp')
- output 11: float32 [960, 2560], P('fsdp')
- output 12: float32 [960, 2560], P('fsdp')
- output 13: float32 [2560, 960], P('fsdp')
All inputs are finite; a program needn't handle non-finite values.
Results may differ from a plain program's by a relative error of at most 0.0180273.
Values are sent between devices in bfloat16 or wider.
A program may use at most 1 GiB of HBM per device.

v0:
```python
import math
import jax
import jax.numpy as jnp
from jax import lax
from jax.sharding import PartitionSpec as P

NORM_EPS = 1e-6
ROPE_THETA = 1.0e6
AXIS_NAME = 'fsdp'
SHARDED = (True, True, True, True, False, False, True, True, True, True, True)


def rope_tables(positions, head_dim):
    half_dim = head_dim // 2
    inv_freq = jnp.exp(jnp.arange(half_dim, dtype=jnp.float32) * (-2.0 * math.log(ROPE_THETA) / head_dim))
    angles = positions.astype(jnp.float32)[:, :, None] * inv_freq
    return jnp.cos(angles), jnp.sin(angles)


def rotate(values, cos_t, sin_t):
    half_dim = values.shape[-1] // 2
    lead_half = values[..., :half_dim]
    tail_half = values[..., half_dim:]
    return jnp.concatenate([lead_half * cos_t - tail_half * sin_t, tail_half * cos_t + lead_half * sin_t], axis=-1)


def norm_fwd(values):
    values_f = values.astype(jnp.float32)
    inv_rms = lax.rsqrt(jnp.mean(values_f * values_f, axis=-1, keepdims=True) + NORM_EPS)
    return values_f * inv_rms, inv_rms


def norm_bwd(grad_out, normed, inv_rms, norm_gain):
    grad_normed = grad_out * norm_gain.astype(jnp.float32)
    mean_term = jnp.mean(grad_normed * normed, axis=-1, keepdims=True)
    return inv_rms * (grad_normed - normed * mean_term)


def attn_fwd(q_rot, k_rot, v_raw):
    seq_len = q_rot.shape[1]
    attn_scale = q_rot.shape[-1] ** -0.5
    scores = jnp.einsum('bqgrh,bkgh->bgrqk', q_rot, k_rot, preferred_element_type=jnp.float32) * attn_scale
    causal = lax.broadcasted_iota(jnp.int32, (seq_len, seq_len), 0) >= lax.broadcasted_iota(jnp.int32, (seq_len, seq_len), 1)
    attn_probs = jax.nn.softmax(jnp.where(causal, scores, -1e30), axis=-1)
    attn_heads = jnp.einsum('bgrqk,bkgh->bqgrh', attn_probs.astype(jnp.bfloat16), v_raw, preferred_element_type=jnp.float32)
    return attn_heads.astype(jnp.bfloat16), attn_probs


def attn_bwd(grad_out, q_rot, k_rot, v_raw, attn_probs):
    attn_scale = q_rot.shape[-1] ** -0.5
    grad_b = grad_out.astype(jnp.bfloat16)
    probs_b = attn_probs.astype(jnp.bfloat16)
    grad_probs = jnp.einsum('bqgrh,bkgh->bgrqk', grad_b, v_raw, preferred_element_type=jnp.float32)
    grad_v = jnp.einsum('bgrqk,bqgrh->bkgh', probs_b, grad_b, preferred_element_type=jnp.float32)
    grad_scores = attn_probs * (grad_probs - jnp.sum(grad_probs * attn_probs, axis=-1, keepdims=True)) * attn_scale
    scores_b = grad_scores.astype(jnp.bfloat16)
    grad_q = jnp.einsum('bgrqk,bkgh->bqgrh', scores_b, k_rot, preferred_element_type=jnp.float32)
    grad_k = jnp.einsum('bgrqk,bqgrh->bkgh', scores_b, q_rot, preferred_element_type=jnp.float32)
    return grad_q, grad_k, grad_v


def layer_fwd(x_emb, positions, weights):
    attn_norm, w_query, w_key, w_value, q_norm, k_norm, w_out, mlp_norm, w_gate, w_up, w_down = weights
    batch_len, seq_len, model_dim = x_emb.shape
    head_dim = q_norm.shape[0]
    kv_heads = w_key.shape[1] // head_dim
    q_per_kv = w_query.shape[1] // w_key.shape[1]
    cos_t, sin_t = rope_tables(positions, head_dim)
    cos_q = cos_t[:, :, None, None, :]
    sin_q = sin_t[:, :, None, None, :]
    cos_k = cos_t[:, :, None, :]
    sin_k = sin_t[:, :, None, :]
    normed1, norm1_inv = norm_fwd(x_emb)
    attn_in = (normed1 * attn_norm.astype(jnp.float32)).astype(jnp.bfloat16)
    q_raw = jnp.einsum('bsd,dn->bsn', attn_in, w_query, preferred_element_type=jnp.float32).astype(jnp.bfloat16).reshape(batch_len, seq_len, kv_heads, q_per_kv, head_dim)
    k_raw = jnp.einsum('bsd,dn->bsn', attn_in, w_key, preferred_element_type=jnp.float32).astype(jnp.bfloat16).reshape(batch_len, seq_len, kv_heads, head_dim)
    v_raw = jnp.einsum('bsd,dn->bsn', attn_in, w_value, preferred_element_type=jnp.float32).astype(jnp.bfloat16).reshape(batch_len, seq_len, kv_heads, head_dim)
    q_normed, q_inv = norm_fwd(q_raw)
    k_normed, k_inv = norm_fwd(k_raw)
    q_rot = rotate(q_normed * q_norm.astype(jnp.float32), cos_q, sin_q).astype(jnp.bfloat16)
    k_rot = rotate(k_normed * k_norm.astype(jnp.float32), cos_k, sin_k).astype(jnp.bfloat16)
    attn_heads, attn_probs = attn_fwd(q_rot, k_rot, v_raw)
    attn_flat = attn_heads.reshape(batch_len, seq_len, -1)
    attn_proj = jnp.einsum('bsn,nd->bsd', attn_flat, w_out, preferred_element_type=jnp.float32)
    hidden = (x_emb.astype(jnp.float32) + attn_proj).astype(jnp.bfloat16)
    normed2, norm2_inv = norm_fwd(hidden)
    mlp_in = (normed2 * mlp_norm.astype(jnp.float32)).astype(jnp.bfloat16)
    gate_pre = jnp.einsum('bsd,df->bsf', mlp_in, w_gate, preferred_element_type=jnp.float32)
    up_proj = jnp.einsum('bsd,df->bsf', mlp_in, w_up, preferred_element_type=jnp.float32)
    mlp_act = (jax.nn.silu(gate_pre) * up_proj).astype(jnp.bfloat16)
    mlp_proj = jnp.einsum('bsf,fd->bsd', mlp_act, w_down, preferred_element_type=jnp.float32)
    layer_out = (hidden.astype(jnp.float32) + mlp_proj).astype(jnp.bfloat16)
    saved_acts = (normed1, norm1_inv, attn_in, q_normed, q_inv, k_normed, k_inv, q_rot, k_rot, v_raw, attn_probs, attn_flat, normed2, norm2_inv, mlp_in, gate_pre, up_proj, mlp_act, cos_q, sin_q, cos_k, sin_k)
    return layer_out, saved_acts


def layer_bwd(dy_out, saved_acts, weights):
    attn_norm, w_query, w_key, w_value, q_norm, k_norm, w_out, mlp_norm, w_gate, w_up, w_down = weights
    (normed1, norm1_inv, attn_in, q_normed, q_inv, k_normed, k_inv, q_rot, k_rot, v_raw, attn_probs, attn_flat, normed2, norm2_inv, mlp_in, gate_pre, up_proj, mlp_act, cos_q, sin_q, cos_k, sin_k) = saved_acts
    batch_len, seq_len, model_dim = dy_out.shape
    grad_w_down = jnp.einsum('bsf,bsd->fd', mlp_act, dy_out, preferred_element_type=jnp.float32)
    grad_act = jnp.einsum('bsd,fd->bsf', dy_out, w_down, preferred_element_type=jnp.float32)
    gate_sig = jax.nn.sigmoid(gate_pre)
    grad_gate = (grad_act * up_proj * gate_sig * (1.0 + gate_pre * (1.0 - gate_sig))).astype(jnp.bfloat16)
    grad_up = (grad_act * gate_pre * gate_sig).astype(jnp.bfloat16)
    grad_w_gate = jnp.einsum('bsd,bsf->df', mlp_in, grad_gate, preferred_element_type=jnp.float32)
    grad_w_up = jnp.einsum('bsd,bsf->df', mlp_in, grad_up, preferred_element_type=jnp.float32)
    grad_mlp_in = jnp.einsum('bsf,df->bsd', grad_gate, w_gate, preferred_element_type=jnp.float32) + jnp.einsum('bsf,df->bsd', grad_up, w_up, preferred_element_type=jnp.float32)
    grad_mlp_norm = jnp.sum(grad_mlp_in * normed2, axis=(0, 1))
    grad_hidden = dy_out.astype(jnp.float32) + norm_bwd(grad_mlp_in, normed2, norm2_inv, mlp_norm)
    hidden_b = grad_hidden.astype(jnp.bfloat16)
    grad_w_out = jnp.einsum('bsn,bsd->nd', attn_flat, hidden_b, preferred_element_type=jnp.float32)
    grad_heads = jnp.einsum('bsd,nd->bsn', hidden_b, w_out, preferred_element_type=jnp.float32).reshape(q_rot.shape)
    grad_q, grad_k, grad_v = attn_bwd(grad_heads, q_rot, k_rot, v_raw, attn_probs)
    grad_qt = rotate(grad_q, cos_q, -sin_q)
    grad_kt = rotate(grad_k, cos_k, -sin_k)
    grad_q_norm = jnp.sum(grad_qt * q_normed, axis=(0, 1, 2, 3))
    grad_k_norm = jnp.sum(grad_kt * k_normed, axis=(0, 1, 2))
    grad_q_raw = norm_bwd(grad_qt, q_normed, q_inv, q_norm).astype(jnp.bfloat16).reshape(batch_len, seq_len, -1)
    grad_k_raw = norm_bwd(grad_kt, k_normed, k_inv, k_norm).astype(jnp.bfloat16).reshape(batch_len, seq_len, -1)
    grad_v_raw = grad_v.astype(jnp.bfloat16).reshape(batch_len, seq_len, -1)
    grad_w_query = jnp.einsum('bsd,bsn->dn', attn_in, grad_q_raw, preferred_element_type=jnp.float32)
    grad_w_key = jnp.einsum('bsd,bsn->dn', attn_in, grad_k_raw, preferred_element_type=jnp.float32)
    grad_w_value = jnp.einsum('bsd,bsn->dn', attn_in, grad_v_raw, preferred_element_type=jnp.float32)
    grad_attn_in = (jnp.einsum('bsn,dn->bsd', grad_q_raw, w_query, preferred_element_type=jnp.float32)
                    + jnp.einsum('bsn,dn->bsd', grad_k_raw, w_key, preferred_element_type=jnp.float32)
                    + jnp.einsum('bsn,dn->bsd', grad_v_raw, w_value, preferred_element_type=jnp.float32))
    grad_attn_norm = jnp.sum(grad_attn_in * normed1, axis=(0, 1))
    grad_x_emb = grad_hidden + norm_bwd(grad_attn_in, normed1, norm1_inv, attn_norm)
    return grad_x_emb, (grad_attn_norm, grad_w_query, grad_w_key, grad_w_value, grad_q_norm, grad_k_norm, grad_w_out, grad_mlp_norm, grad_w_gate, grad_w_up, grad_w_down)


def solution(mesh):
    row_spec = P(AXIS_NAME, None)
    vec_spec = P(AXIS_NAME)
    full_spec = P(None)
    batch_spec = P(AXIS_NAME, None, None)
    weight_specs = (vec_spec, row_spec, row_spec, row_spec, full_spec, full_spec, row_spec, vec_spec, row_spec, row_spec, row_spec)

    def device_step(tokens, positions, table_shard, attn_norm, w_query, w_key, w_value, q_norm, k_norm, w_out, mlp_norm, w_gate, w_up, w_down, dy_out):
        shards = (attn_norm, w_query, w_key, w_value, q_norm, k_norm, w_out, mlp_norm, w_gate, w_up, w_down)
        weights = tuple(lax.all_gather(w_shard, AXIS_NAME, tiled=True) if is_sharded else w_shard for w_shard, is_sharded in zip(shards, SHARDED))
        batch_len, seq_len = tokens.shape
        rows_local, model_dim = table_shard.shape
        all_ids = lax.all_gather(tokens.reshape(-1), AXIS_NAME, tiled=True)
        local_ids = all_ids - lax.axis_index(AXIS_NAME) * rows_local
        is_owner = (local_ids >= 0) & (local_ids < rows_local)
        picked = jnp.take(table_shard, jnp.clip(local_ids, 0, rows_local - 1), axis=0)
        picked = jnp.where(is_owner[:, None], picked, jnp.zeros((), picked.dtype))
        x_emb = lax.psum_scatter(picked, AXIS_NAME, scatter_dimension=0, tiled=True).reshape(batch_len, seq_len, model_dim)
        layer_out, saved_acts = layer_fwd(x_emb, positions, weights)
        grad_x_emb, grad_full = layer_bwd(dy_out, saved_acts, weights)
        grad_shards = tuple(lax.psum_scatter(grad_part, AXIS_NAME, scatter_dimension=0, tiled=True) if is_sharded else lax.psum(grad_part, AXIS_NAME) for grad_part, is_sharded in zip(grad_full, SHARDED))
        all_rows = lax.all_gather(grad_x_emb.reshape(-1, model_dim), AXIS_NAME, tiled=True)
        d_table = jax.ops.segment_sum(all_rows, jnp.where(is_owner, local_ids, rows_local), num_segments=rows_local)
        return (layer_out, d_table) + grad_shards

    return jax.shard_map(device_step, mesh=mesh, in_specs=(row_spec, row_spec, row_spec) + weight_specs + (batch_spec,), out_specs=(batch_spec, row_spec) + weight_specs, check_vma=False)
```

profile of v0, /device:TPU:0, one launch (start us, length us, event | category | flops | bytes accessed | tf_op | source)
XLA Modules:
  0.0 1598.2 jit_solution(5961524288392090173)
XLA Ops:
  10.0 43.5 %all-gather = s32[1,16384]{1,0:T(1,128)S(1)} all-gather(s32[1,512]{1,0:T(1,128)} %param.15), channel_id=2, replica_groups=mesh['fsdp'=32] {'fsdp'}, dimensions={1}, use_global_device_ids=true | all-gather | bytes 67584 | tf_op jit(solution)/shard_map/all_gather | solution.py:145
  57.4 69.6 %gather_fusion = bf16[16384,960]{1,0:T(8,128)(2,1)} fusion(bf16[1536,960]{1,0:T(8,128)(2,1)S(1)} %copy.50, s32[16384]{0:T(1024)S(1)} %get-tuple-element.94), kind=kCustom, calls=%fused_computation | custom fusion | bytes 62980096 | tf_op jit(solution)/shard_map/jit(_take)/gather | solution.py:148
  126.9 39.4 %copy.51 = bf16[16384,960]{0,1:T(8,128)(2,1)} copy(bf16[16384,960]{1,0:T(8,128)(2,1)} %gather_fusion) | data formatting | bytes 62914560 | tf_op jit(solution)/shard_map/jit(_take)/gather | solution.py:148
  166.4 21.8 %select_select_fusion = bf16[16384,960]{0,1:T(8,128)(2,1)} fusion(bf16[16384,960]{0,1:T(8,128)(2,1)} %copy.51, pred[16384]{0:T(1024)(128)(4,1)S(1)} %get-tuple-element.96, pred[16384]{0:T(1024)(128)(4,1)S(1)} %get-tuple-element.95), kind=kLoop, calls=%fused_computation.2 | loop fusion | flops 31457280 | bytes 62947328 | tf_op jit(solution)/shard_map/jit(_where)/select_n | solution.py:149
  189.6 37.2 %all-reduce.17 = (bf16[960]{0:T(1024)(128)(2,1)S(1)}, bf16[960]{0:T(1024)(128)(2,1)S(1)}) all-reduce(bf16[960]{0:T(1024)(128)(2,1)S(1)} %dynamic-update-slice, bf16[960]{0:T(1024)(128)(2,1)S(1)} %dynamic-update-slice.1), channel_id=1, replica_groups=mesh['fsdp'=32] {'fsdp'}, use_global_device_ids=true, to_apply=%add | all-reduce | flops 1920 | bytes 7680
  228.2 44.5 %all-gather.3 = bf16[32,30,320]{2,1,0:T(8,128)(2,1)S(1)} all-gather(bf16[1,30,320]{2,1,0:T(8,128)(2,1)S(1)} %bitcast.222), channel_id=1, replica_groups=mesh['fsdp'=32] {'fsdp'}, dimensions={0}, use_global_device_ids=true | all-gather | bytes 633600 | tf_op jit(solution)/shard_map/all_gather | solution.py:142
  273.9 38.7 %all-gather.2 = bf16[32,30,320]{2,1,0:T(8,128)(2,1)S(1)} all-gather(bf16[1,30,320]{2,1,0:T(8,128)(2,1)S(1)} %bitcast.223), channel_id=1, replica_groups=mesh['fsdp'=32] {'fsdp'}, dimensions={0}, use_global_device_ids=true | all-gather | bytes 633600 | tf_op jit(solution)/shard_map/all_gather | solution.py:142
  324.0 7.5 reshape.795
  331.5 7.6 reshape.797
  339.1 210.3 %reduce-scatter.15.cloned.1.call-done = bf16[512,960]{0,1:T(8,128)(2,1)} async-done(((bf16[16384,960]{0,1:T(8,128)(2,1)}), bf16[512,960]{0,1:T(8,128)(2,1)}) %reduce-scatter.15.cloned.1.call-update) | async-done | bytes 983056 | tf_op jit(solution)/shard_map/reduce_scatter | solution.py:150
  556.7 6.9 fusion.12
  563.6 8.7 fusion.11
  572.4 8.3 fusion.49
  591.9 25.3 %all-gather.15.cloned.1.call-done = bf16[2560,960]{1,0:T(8,128)(2,1)} async-done(((bf16[80,960]{1,0:T(8,128)(2,1)}), bf16[2560,960]{1,0:T(8,128)(2,1)}) %all-gather.15.cloned.1.call-update) | async-done | bytes 4915216 | tf_op jit(solution)/shard_map/all_gather | solution.py:142
  617.2 10.5 multiply_convert_fusion
  647.9 8.5 fusion.6
  656.4 9.0 fusion.13
  680.7 8.8 fusion.64
  711.7 522.5 %fusion.101 = (f32[32,960]{1,0:T(8,128)S(1)}, f32[32,320]{1,0:T(8,128)}, f32[32,320]{1,0:T(8,128)}, f32[32,960]{1,0:T(8,128)S(1)}, f32[32,2560]{1,0:T(8,128)}, /*index=5*/f32[32,2560]{1,0:T(8,128)S(1)}) fusion(f32[960,960]{1,0:T(8,128)} %fusion.96, f32[960,320]{1,0:T(8,128)} %fusion.94, f32[960,320]{1,0:T(8,128)} %fusion.92, f32[960,960]{1,0:T(8,128)} %fusion.62, ...), kind=kCustom, calls=%all-reduce-scatter.6 | all-reduce-scatter fusion | flops 7864321 | bytes 30474240
  1253.7 21.0 %collective-permute-start.7 = (f32[30,960]{1,0:T(8,128)S(1)}, f32[30,960]{1,0:T(8,128)}, u32[]{:S(2)}, u32[]{:S(2)}) collective-permute-start(f32[30,960]{1,0:T(8,128)S(1)} %slice.45), channel_id=1, source_target_pairs={{0,2},{1,3},{2,4},{3,5},{4,6},{5,7},{6,8},{7,9},{8,10},{9,11},{10,... | collective-permute-start | bytes 345608
  1276.5 47.5 %all-reduce.16 = (f32[960]{0:T(1024)S(1)}, f32[64]{0:T(128)}, f32[64]{0:T(128)}, f32[960]{0:T(1024)S(1)}) all-reduce(f32[960]{0:T(1024)S(1)} %get-tuple-element.54, f32[64]{0:T(128)S(1)} %reduce_sum.153, f32[64]{0:T(128)S(1)} %reduce_sum.156, f32[960]{0:T(1024)S(1)} %get-tuple-element.52), channel_id=5, replica_groups=mesh['fsdp'=32] {'fsdp'}, use_global_device_ids=true, to_apply=%region_14.15.clone | all-reduce | flops 2048 | bytes 16384
  1352.4 20.5 %collective-permute-done.9 = f32[30,2560]{1,0:T(8,128)} collective-permute-done((f32[30,2560]{1,0:T(8,128)S(1)}, f32[30,2560]{1,0:T(8,128)}, u32[]{:S(2)}, u32[]{:S(2)}) %collective-permute-start.9) | collective-permute-done | bytes 307232
  1376.8 64.6 %copy.56 = f32[16384,960]{1,0:T(8,128)} copy(f32[16384,960]{0,1:T(8,128)} %bitcast.197) | data formatting | bytes 125829120 | tf_op jit(solution)/shard_map/all_gather | solution.py:154
  1441.4 143.3 %scatter_custom_fusion = f32[1536,960]{1,0:T(8,128)} fusion(s32[16384]{0:T(1024)} %get-tuple-element.93, f32[16384,960]{1,0:T(8,128)} %copy.56, f32[]{:T(128)} %constant.22.clone.1), kind=kCustom, calls=%fused_computation.24 | custom fusion | flops 15728640 | bytes 5898752 | tf_op jit(solution)/shard_map/scatter-add | solution.py:155
  (296 shorter events, 157.0 us)
Async XLA Ops:
  7.2 306.8 %all-gather.21.cloned.1.call-start = ((), (), s32[]{:S(2)}) async-start(), calls=%async_computation.7 | async-start | bytes 2162688 | tf_op jit(solution)/shard_map/all_gather | solution.py:142
  7.9 312.1 %all-gather.19.cloned.1.call-start = ((), (), s32[]{:S(2)}) async-start(), calls=%async_computation.6 | async-start | bytes 2162688 | tf_op jit(solution)/shard_map/all_gather | solution.py:142
  8.7 315.3 %all-gather.23.cloned.1.call-start = ((), (), s32[]{:S(2)}) async-start(), calls=%async_computation.8 | async-start | bytes 5406720 | tf_op jit(solution)/shard_map/all_gather | solution.py:142
  9.4 322.1 %all-gather.25.cloned.1.call-start = ((), (), s32[]{:S(2)}) async-start(), calls=%async_computation.9 | async-start | bytes 5406720 | tf_op jit(solution)/shard_map/all_gather | solution.py:142
  10.0 539.4 %reduce-scatter.15.cloned.1.call-start = ((), (), s32[]{:S(2)}) async-start(), calls=%async_computation.2 | async-start | bytes 32440320 | tf_op jit(solution)/shard_map/reduce_scatter | solution.py:150
  188.3 428.9 %all-gather.15.cloned.1.call-start = ((), (), s32[]{:S(2)}) async-start(), calls=%async_computation.3 | async-start | bytes 5406720 | tf_op jit(solution)/shard_map/all_gather | solution.py:142
  188.8 1188.0 %all-gather.17.cloned.1.call-start = ((), (), s32[]{:S(2)}) async-start(), calls=%async_computation.5 | async-start | bytes 64880640 | tf_op jit(solution)/shard_map/all_gather | solution.py:154
  189.0 366.8 %copy-start.56 = (f32[64]{0:T(128)}, f32[64]{0:T(128)S(1)}, u32[]{:S(2)}) copy-start(f32[64]{0:T(128)S(1)} %convert_element_type.206) | copy-start | bytes 772
  189.1 365.7 %copy-start.54 = (f32[64]{0:T(128)}, f32[64]{0:T(128)S(1)}, u32[]{:S(2)}) copy-start(f32[64]{0:T(128)S(1)} %convert_element_type.201) | copy-start | bytes 772
  226.8 328.2 %copy-start.46 = (f32[960]{0:T(1024)}, f32[960]{0:T(1024)S(1)}, u32[]{:S(2)}) copy-start(f32[960]{0:T(1024)S(1)} %convert_element_type.195) | copy-start | bytes 11524
  313.9 242.4 %copy-start.29 = (f32[512,32]{0,1:T(8,128)}, f32[512,32]{0,1:T(8,128)S(1)}, u32[]{:S(2)}) copy-start(f32[512,32]{0,1:T(8,128)S(1)} %get-tuple-element.99) | copy-start | bytes 196612
  680.4 910.7 %reduce-scatter.17.cloned.1.call-start = ((), (), s32[]{:S(2)}) async-start(), calls=%async_computation.4 | async-start | bytes 10813440 | tf_op jit(solution)/shard_map/reduce_scatter | solution.py:153
  1235.9 89.4 %collective-permute-start.2 = (f32[32,320]{1,0:T(8,128)}, f32[32,320]{1,0:T(8,128)}, u32[]{:S(2)}, u32[]{:S(2)}) collective-permute-start(f32[32,320]{1,0:T(8,128)} %get-tuple-element.69), channel_id=1, source_target_pairs={{0,1},{1,2},{2,3},{3,4},{4,5},{5,6},{6,7},{7,8},{8,9},{9,10},{10,1... | collective-permute-start | bytes 122888
  1239.2 90.0 %collective-permute-start.5 = (f32[30,320]{1,0:T(8,128)}, f32[30,320]{1,0:T(8,128)}, u32[]{:S(2)}, u32[]{:S(2)}) collective-permute-start(f32[30,320]{1,0:T(8,128)} %slice.44), channel_id=1, source_target_pairs={{0,2},{1,3},{2,4},{3,5},{4,6},{5,7},{6,8},{7,9},{8,10},{9,11},{10,... | collective-permute-start | bytes 115208
  1241.1 33.7 %collective-permute-start.3 = (f32[30,320]{1,0:T(8,128)}, f32[30,320]{1,0:T(8,128)}, u32[]{:S(2)}, u32[]{:S(2)}) collective-permute-start(f32[30,320]{1,0:T(8,128)} %slice.43), channel_id=1, source_target_pairs={{0,2},{1,3},{2,4},{3,5},{4,6},{5,7},{6,8},{7,9},{8,10},{9,11},{10,... | collective-permute-start | bytes 115208
  1243.0 100.9 %collective-permute-start = (f32[32,960]{1,0:T(8,128)S(1)}, f32[32,960]{1,0:T(8,128)}, u32[]{:S(2)}, u32[]{:S(2)}) collective-permute-start(f32[32,960]{1,0:T(8,128)S(1)} %get-tuple-element.68), channel_id=1, source_target_pairs={{0,1},{1,2},{2,3},{3,4},{4,5},{5,6},{6,7},{7,8},{8,9},{9,10},{10,1... | collective-permute-start | bytes 368648
  1253.7 83.5 %collective-permute-start.7 = (f32[30,960]{1,0:T(8,128)S(1)}, f32[30,960]{1,0:T(8,128)}, u32[]{:S(2)}, u32[]{:S(2)}) collective-permute-start(f32[30,960]{1,0:T(8,128)S(1)} %slice.45), channel_id=1, source_target_pairs={{0,2},{1,3},{2,4},{3,5},{4,6},{5,7},{6,8},{7,9},{8,10},{9,11},{10,... | collective-permute-start | bytes 345608
  1274.7 66.2 %collective-permute-start.1 = (f32[30,960]{1,0:T(8,128)S(1)}, f32[30,960]{1,0:T(8,128)S(1)}, u32[]{:S(2)}, u32[]{:S(2)}) collective-permute-start(f32[30,960]{1,0:T(8,128)S(1)} %slice.42), channel_id=1, source_target_pairs={{0,2},{1,3},{2,4},{3,5},{4,6},{5,7},{6,8},{7,9},{8,10},{9,11},{10,... | collective-permute-start | bytes 345608
  1325.2 9.6 collective-permute-start.4
  1329.2 19.8 %collective-permute-start.6 = (f32[32,960]{1,0:T(8,128)S(1)}, f32[32,960]{1,0:T(8,128)}, u32[]{:S(2)}, u32[]{:S(2)}) collective-permute-start(f32[32,960]{1,0:T(8,128)S(1)} %get-tuple-element.71), channel_id=1, source_target_pairs={{0,1},{1,2},{2,3},{3,4},{4,5},{5,6},{6,7},{7,8},{8,9},{9,10},{10,1... | collective-permute-start | bytes 368648
  1334.8 38.1 %collective-permute-start.8 = (f32[32,2560]{1,0:T(8,128)S(1)}, f32[32,2560]{1,0:T(8,128)S(1)}, u32[]{:S(2)}, u32[]{:S(2)}) collective-permute-start(f32[32,2560]{1,0:T(8,128)S(1)} %copy-done.15), channel_id=1, source_target_pairs={{0,1},{1,2},{2,3},{3,4},{4,5},{5,6},{6,7},{7,8},{8,9},{9,10},{10,1... | collective-permute-start | bytes 983048
  1337.2 37.3 %collective-permute-start.10 = (f32[32,2560]{1,0:T(8,128)S(1)}, f32[32,2560]{1,0:T(8,128)S(1)}, u32[]{:S(2)}, u32[]{:S(2)}) collective-permute-start(f32[32,2560]{1,0:T(8,128)S(1)} %get-tuple-element.73), channel_id=1, source_target_pairs={{0,1},{1,2},{2,3},{3,4},{4,5},{5,6},{6,7},{7,8},{8,9},{9,10},{10,1... | collective-permute-start | bytes 983048
  1341.0 33.6 %collective-permute-start.11 = (f32[30,2560]{1,0:T(8,128)S(1)}, f32[30,2560]{1,0:T(8,128)S(1)}, u32[]{:S(2)}, u32[]{:S(2)}) collective-permute-start(f32[30,2560]{1,0:T(8,128)S(1)} %slice.47), channel_id=1, source_target_pairs={{0,2},{1,3},{2,4},{3,5},{4,6},{5,7},{6,8},{7,9},{8,10},{9,11},{10,... | collective-permute-start | bytes 921608
  1343.8 29.1 %collective-permute-start.9 = (f32[30,2560]{1,0:T(8,128)S(1)}, f32[30,2560]{1,0:T(8,128)}, u32[]{:S(2)}, u32[]{:S(2)}) collective-permute-start(f32[30,2560]{1,0:T(8,128)S(1)} %slice.46), channel_id=1, source_target_pairs={{0,2},{1,3},{2,4},{3,5},{4,6},{5,7},{6,8},{7,9},{8,10},{9,11},{10,... | collective-permute-start | bytes 921608
  (72 other events, 1111.0 us)
Sparse Core Ops, SparseCore 0:
  10.8 58.9 all-gather.20
  72.7 55.1 all-gather.18
  130.7 64.3 all-gather.22
  197.8 66.8 all-gather.24
  271.0 278.3 reduce-scatter.14
  552.1 65.0 all-gather.14
  680.6 556.0 all-gather.16
  1239.5 182.2 reduce-scatter.16
where the time goes:
time: 1620 us; the launch traced here: 1600 us
  blocking collectives  734 us (45%)
  waiting for transfers between devices  259 us (16%)
  local copies, waits for them, and re-layouts  232 us (14%)
  other arithmetic  196 us (12%)
  matrix products  112 us (7%)
  starting transfers between devices  49.4 us (3%)
    unnamed x3, blocking collectives  607 us
    reduce_scatter x1, waiting for transfers between devices, device_step(): lax.psum_scatter(picked, AXIS_NAME, scatter_dimension=0, tiled=True)  210 us
    scatter-add x1, other arithmetic, device_step(): jax.ops.segment_sum(all_rows, jnp.where(is_owner, local_ids, rows_local),...  143 us
    gather x2, local copies, waits for them, and re-layouts, device_step(): jnp.take(table_shard, jnp.clip(local_ids, 0, rows_local - 1), axis=0)  109 us
    all_gather x2, blocking collectives, device_step(): lax.all_gather(w_shard, AXIS_NAME, tiled=True)  83.2 us
    all_gather x1, local copies, waits for them, and re-layouts, device_step(): lax.all_gather(grad_x_emb.reshape(-1, model_dim), AXIS_NAME, tiled=True)  64.6 us
    unnamed x184, local copies, waits for them, and re-layouts  52.9 us
    unnamed x12, starting transfers between devices  48.9 us
  transfers between devices with their start and end apart: 20, of which 3 were waited for; matrix products, arithmetic and copies ran while one was open for 63% of the time, Pallas kernels for 0%

commit v1 on v0

v1 whole, which is shorter than its diff:
```python
import functools
import math
import jax
import jax.numpy as jnp
from jax import lax
from jax.experimental import pallas as pl
from jax.experimental.pallas import tpu as pltpu
from jax.sharding import PartitionSpec as P

NORM_EPS = 1e-6
ROPE_THETA = 1.0e6
AXIS_NAME = 'fsdp'
MESH = pl.DeviceIdType.MESH
NZ, NQ, NC = 4, 4, 2
N_DEV = NZ * NQ * NC
LANES = 128
SUBL = 8
VMEM_BYTES = 62 * 1024 * 1024
J_GATHER = (0, 1, 3, 2)
J_SCATTER = (2, 1, 3, 0)


def dev_id(z, q, c):
    y = lax.div(q, 2)
    x = lax.rem(q + y, 2)
    return z * 8 + y * 4 + x * 2 + c


def my_coords():
    me = lax.axis_index(AXIS_NAME)
    z = lax.div(me, 8)
    y = lax.rem(lax.div(me, 4), 2)
    x = lax.rem(lax.div(me, 2), 2)
    c = lax.rem(me, 2)
    q = y * 2 + lax.rem(x + y, 2)
    return me, z, q, c


def wrap4(value):
    return lax.rem(value + 16, 4)


def entry_barrier(z, q, c):
    barrier = pltpu.get_barrier_semaphore()
    peers = [dev_id(wrap4(z + k), q, c) for k in (1, 2, 3)]
    peers += [dev_id(z, wrap4(q + 1), c), dev_id(z, wrap4(q + 3), c), dev_id(z, q, 1 - c)]
    for peer in peers:
        pl.semaphore_signal(barrier, inc=1, device_id=(peer,), device_id_type=MESH)
    pl.semaphore_wait(barrier, len(peers))


def ids_kernel(src, dst, loc_sem, send_sem, recv_sem):
    me = lax.axis_index(AXIS_NAME)
    barrier = pltpu.get_barrier_semaphore()

    @pl.loop(1, N_DEV)
    def _(k):
        pl.semaphore_signal(barrier, inc=1, device_id=(lax.rem(me + k, N_DEV),), device_id_type=MESH)
    pl.semaphore_wait(barrier, N_DEV - 1)
    local = pltpu.make_async_copy(src, dst.at[me], loc_sem)
    local.start()

    @pl.loop(1, N_DEV)
    def _(k):
        pltpu.make_async_remote_copy(src_ref=src, dst_ref=dst.at[me], send_sem=send_sem.at[k], recv_sem=recv_sem.at[k],
                                     device_id=(lax.rem(me + k, N_DEV),), device_id_type=MESH).start()
    local.wait()

    @pl.loop(1, N_DEV)
    def _(k):
        copy = pltpu.make_async_remote_copy(src_ref=src, dst_ref=dst.at[lax.rem(me + N_DEV - k, N_DEV)], send_sem=send_sem.at[k],
                                            recv_sem=recv_sem.at[k], device_id=(lax.rem(me + k, N_DEV),), device_id_type=MESH)
        copy.wait_send()
        copy.wait_recv()


def gather_ids(block):
    return pl.pallas_call(
        ids_kernel,
        out_shape=jax.ShapeDtypeStruct((N_DEV,) + block.shape, block.dtype),
        in_specs=[pl.BlockSpec(memory_space=pltpu.VMEM)],
        out_specs=pl.BlockSpec(memory_space=pltpu.VMEM),
        scratch_shapes=[pltpu.SemaphoreType.DMA, pltpu.SemaphoreType.DMA((N_DEV,)), pltpu.SemaphoreType.DMA((N_DEV,))],
        compiler_params=pltpu.CompilerParams(collective_id=0, has_side_effects=True),
        name='gather_ids',
    )(block)


def weights_kernel(n_arr, *refs):
    ins = refs[:n_arr]
    outs = refs[n_arr:2 * n_arr]
    loc_sem, z_send, z_recv, r_send, r_recv, p_send, p_recv = refs[2 * n_arr:]
    me, z, q, c = my_coords()
    step_dir = 1 - 2 * c
    nxt = dev_id(z, wrap4(q + step_dir), c)
    mate = dev_id(z, q, 1 - c)
    entry_barrier(z, q, c)

    def remote(src, dst, send, recv, target):
        return pltpu.make_async_remote_copy(src_ref=src, dst_ref=dst, send_sem=send, recv_sem=recv, device_id=(target,), device_id_type=MESH)

    def block_at(j, s):
        return dev_id(wrap4(z - j), wrap4(q - step_dir * s), c)

    def source(a, j, s):
        return ins[a] if (j, s) == (0, 0) else outs[a].at[block_at(j, s)]

    def ring(a, j, s):
        return remote(source(a, j, s), outs[a].at[block_at(j, s)], r_send.at[a, s, j], r_recv.at[a, s, j], nxt)

    def ring_in(a, j, s):
        dst = outs[a].at[block_at(j, s + 1)]
        return remote(dst, dst, r_send.at[a, s, j], r_recv.at[a, s, j], nxt)

    def pair(a, j, s):
        return remote(source(a, j, s), outs[a].at[block_at(j, s)], p_send.at[a, s, j], p_recv.at[a, s, j], mate)

    def pair_in(a, j, s):
        dst = outs[a].at[dev_id(wrap4(z - j), wrap4(q + step_dir * s), 1 - c)]
        return remote(dst, dst, p_send.at[a, s, j], p_recv.at[a, s, j], mate)

    def column(a, k):
        return remote(ins[a], outs[a].at[me], z_send.at[a, k - 1], z_recv.at[a, k - 1], dev_id(wrap4(z + k), q, c))

    def column_in(a, k):
        dst = outs[a].at[dev_id(wrap4(z - k), q, c)]
        return remote(dst, dst, z_send.at[a, k - 1], z_recv.at[a, k - 1], dev_id(wrap4(z + k), q, c))

    arrays = range(n_arr)
    local = [pltpu.make_async_copy(ins[a], outs[a].at[me], loc_sem.at[a]) for a in arrays]
    for a in arrays:
        ring(a, 0, 0).start()
    for k in (1, 3, 2):
        for a in arrays:
            column(a, k).start()
    for a in arrays:
        local[a].start()
        pair(a, 0, 0).start()

    groups = [(0, 0)]
    for pos, j in enumerate(J_GATHER):
        groups += [(j, 1), (j, 2)]
        if pos + 1 < NZ:
            groups.append((J_GATHER[pos + 1], 0))
        groups.append((j, 3))
    for j, s in groups[1:]:
        for a in arrays:
            if s == 0:
                column_in(a, j).wait_recv()
            else:
                ring_in(a, j, s - 1).wait_recv()
            if s < 3:
                ring(a, j, s).start()
            pair(a, j, s).start()
    for a in arrays:
        local[a].wait()
        for j in range(NZ):
            for s in range(4):
                pair_in(a, j, s).wait_recv()
                pair(a, j, s).wait_send()
                if s < 3:
                    ring(a, j, s).wait_send()
        for k in (1, 2, 3):
            column(a, k).wait_send()


def gather_blocks(blocks, collective_id, name):
    n_arr = len(blocks)
    out_shape = tuple(jax.ShapeDtypeStruct((N_DEV,) + b.shape, b.dtype) for b in blocks)
    dma = pltpu.SemaphoreType.DMA
    return pl.pallas_call(
        functools.partial(weights_kernel, n_arr),
        out_shape=out_shape,
        in_specs=[pl.BlockSpec(memory_space=pltpu.VMEM)] * n_arr,
        out_specs=tuple(pl.BlockSpec(memory_space=pl.ANY) for _ in blocks),
        scratch_shapes=[dma((n_arr,)), dma((n_arr, 3)), dma((n_arr, 3)), dma((n_arr, 3, 4)), dma((n_arr, 3, 4)), dma((n_arr, 4, 4)), dma((n_arr, 4, 4))],
        compiler_params=pltpu.CompilerParams(collective_id=collective_id, has_side_effects=True, vmem_limit_bytes=8 * 1024 * 1024),
        name=name,
    )(*blocks)


def grads_kernel(n_arr, *refs):
    ins = refs[:n_arr]
    outs = refs[n_arr:2 * n_arr]
    scratch = refs[2 * n_arr:]
    own, mbuf, rbuf, zbuf = (scratch[i * n_arr:(i + 1) * n_arr] for i in range(4))
    o_sem, z_send, z_recv, r_send, r_recv, p_send, p_recv = scratch[4 * n_arr:]
    me, z, q, c = my_coords()
    step_dir = 1 - 2 * c
    nxt = dev_id(z, wrap4(q + step_dir), c)
    mate = dev_id(z, q, 1 - c)
    arrays = range(n_arr)
    groups = []
    for pos, j in enumerate(J_SCATTER):
        if pos == 0:
            groups.append((j, 0))
        groups += [(j, 1), (j, 2)]
        if pos + 1 < NZ:
            groups.append((J_SCATTER[pos + 1], 0))
        groups.append((j, 3))
    n_groups = len(groups)

    def remote(src, dst, send, recv, target):
        return pltpu.make_async_remote_copy(src_ref=src, dst_ref=dst, send_sem=send, recv_sem=recv, device_id=(target,), device_id_type=MESH)

    def own_load(g, a):
        j, s = groups[g]
        block = dev_id(wrap4(z + j), wrap4(q - step_dir * (1 + s)), c)
        return pltpu.make_async_copy(ins[a].at[block], own[a].at[g % 2], o_sem.at[a, g % 2])

    def pair(g, a):
        j, s = groups[g]
        block = dev_id(wrap4(z + j), wrap4(q + step_dir * (1 + s)), 1 - c)
        return remote(ins[a].at[block], mbuf[a].at[g], p_send.at[a, g], p_recv.at[a, g], mate)

    def place(j, s):
        return j * 3 + s

    def ring(g, a):
        j, s = groups[g]
        src = mbuf[a].at[g] if s == 0 else rbuf[a].at[place(j, s - 1)]
        return remote(src, rbuf[a].at[place(j, s)], r_send.at[a, place(j, s)], r_recv.at[a, place(j, s)], nxt)

    def column(a, j):
        return remote(rbuf[a].at[place(j, 2)], zbuf[a].at[j - 1], z_send.at[a, j - 1], z_recv.at[a, j - 1], dev_id(wrap4(z + j), q, c))

    def add_into(dst, others):
        rows = dst.shape[0]

        @pl.loop(0, rows // SUBL)
        def _(r):
            here = pl.ds(pl.multiple_of(r * SUBL, SUBL), SUBL)
            total = dst[here, :]
            for other in others:
                total = total + other[here, :]
            dst[here, :] = total

    for a in arrays:
        own_load(0, a).start()
    entry_barrier(z, q, c)
    for g in range(3):
        for a in arrays:
            pair(g, a).start()
    for g, (j, s) in enumerate(groups):
        for a in arrays:
            if g + 1 < n_groups:
                own_load(g + 1, a).start()
            if g + 3 < n_groups:
                pair(g + 3, a).start()
        for a in arrays:
            own_load(g, a).wait()
            pair(g, a).wait_recv()
            if s == 0:
                add_into(mbuf[a].at[g], [own[a].at[g % 2]])
            else:
                slot = place(j, s - 1)
                remote(rbuf[a].at[slot], rbuf[a].at[slot], r_send.at[a, slot], r_recv.at[a, slot], nxt).wait_recv()
                add_into(rbuf[a].at[slot], [own[a].at[g % 2], mbuf[a].at[g]])
            if s < 3:
                ring(g, a).start()
            elif j != 0:
                column(a, j).start()
    for a in arrays:
        for j in (1, 2, 3):
            column(a, j).wait_recv()
        rows = outs[a].shape[0]

        @pl.loop(0, rows // SUBL)
        def _(r):
            here = pl.ds(pl.multiple_of(r * SUBL, SUBL), SUBL)
            total = rbuf[a][place(0, 2), here, :]
            for k in range(3):
                total = total + zbuf[a][k, here, :]
            outs[a][here, :] = total
    for a in arrays:
        for g, (j, s) in enumerate(groups):
            pair(g, a).wait_send()
            if s < 3:
                ring(g, a).wait_send()
        for j in (1, 2, 3):
            column(a, j).wait_send()


def scatter_grads(parts):
    n_arr = len(parts)
    shapes = [p.shape[1:] for p in parts]
    dma = pltpu.SemaphoreType.DMA

    def bufs(count):
        return [pltpu.VMEM((count,) + s, jnp.float32) for s in shapes]

    return pl.pallas_call(
        functools.partial(grads_kernel, n_arr),
        out_shape=tuple(jax.ShapeDtypeStruct(s, jnp.float32) for s in shapes),
        in_specs=[pl.BlockSpec(memory_space=pl.ANY)] * n_arr,
        out_specs=tuple(pl.BlockSpec(memory_space=pltpu.VMEM) for _ in parts),
        scratch_shapes=bufs(2) + bufs(16) + bufs(12) + bufs(3) + [
            dma((n_arr, 2)), dma((n_arr, 3)), dma((n_arr, 3)), dma((n_arr, 12)), dma((n_arr, 12)), dma((n_arr, 16)), dma((n_arr, 16))],
        compiler_params=pltpu.CompilerParams(collective_id=2, has_side_effects=True, vmem_limit_bytes=VMEM_BYTES),
        name='scatter_grads',
    )(*parts)


X_CHUNKS = 4


def rows_kernel(ids, table, out, tab, first, rbuf, zbuf, loc_sem, t_send, t_recv, z_send, z_recv, r_send, r_recv):
    me, z, q, c = my_coords()
    step_dir = 1 - 2 * c
    nxt = dev_id(z, wrap4(q + step_dir), c)
    mate = dev_id(z, q, 1 - c)
    n_local = table.shape[0]
    seq = out.shape[0]
    step = seq // X_CHUNKS
    groups = []
    for pos, j in enumerate(J_SCATTER):
        if pos == 0:
            groups.append((j, 0))
        groups += [(j, 1), (j, 2)]
        if pos + 1 < NZ:
            groups.append((J_SCATTER[pos + 1], 0))
        groups.append((j, 3))

    def remote(src, dst, send, recv, target):
        return pltpu.make_async_remote_copy(src_ref=src, dst_ref=dst, send_sem=send, recv_sem=recv, device_id=(target,), device_id_type=MESH)

    mine = tab.at[pl.ds(c * n_local, n_local)]
    local = pltpu.make_async_copy(table, mine, loc_sem)
    local.start()
    entry_barrier(z, q, c)
    share = remote(table, mine, t_send, t_recv, mate)
    share.start()
    local.wait()
    theirs = tab.at[pl.ds((1 - c) * n_local, n_local)]
    remote(table, theirs, t_send, t_recv, mate).wait_recv()

    def place(j, s):
        return j * 3 + s

    def part(ref, h):
        return ref.at[pl.ds(h * step, step)]

    def ring(j, s, h):
        src = first.at[j] if s == 0 else rbuf.at[place(j, s - 1)]
        return remote(part(src, h), part(rbuf.at[place(j, s)], h), r_send.at[place(j, s), h], r_recv.at[place(j, s), h], nxt)

    def column(j, h):
        return remote(part(rbuf.at[place(j, 2)], h), part(zbuf.at[j - 1], h), z_send.at[j - 1, h], z_recv.at[j - 1, h], dev_id(wrap4(z + j), q, c))

    for j, s in groups:
        block = dev_id(wrap4(z + j), wrap4(q - step_dir * (1 + s)), c)
        for h in range(X_CHUNKS):
            if s > 0:
                slot = place(j, s - 1)
                landed = part(rbuf.at[slot], h)
                remote(landed, landed, r_send.at[slot, h], r_recv.at[slot, h], nxt).wait_recv()
                dst = rbuf.at[slot]
            else:
                dst = first.at[j]

            @pl.loop(0, step // SUBL)
            def _(t):
                for u in range(SUBL):
                    k = h * step + t * SUBL + u
                    row = ids[block * seq + k]
                    held = jnp.logical_and(row >= 0, row < 2 * n_local)
                    value = tab[jnp.clip(row, 0, 2 * n_local - 1)]
                    base = jnp.zeros_like(value) if s == 0 else dst[k]
                    dst[k] = jnp.where(held, value, base)
            if s < 3:
                ring(j, s, h).start()
            elif j != 0:
                column(j, h).start()
    for h in range(X_CHUNKS):
        for j in (1, 2, 3):
            column(j, h).wait_recv()

        @pl.loop(0, step // SUBL)
        def _(t):
            here = pl.ds(h * step + t * SUBL, SUBL)
            total = rbuf[place(0, 2), here]
            for k in range(3):
                total = total + zbuf[k, here]
            out[here] = total
    for h in range(X_CHUNKS):
        for j in range(NZ):
            for s in range(3):
                ring(j, s, h).wait_send()
        for j in (1, 2, 3):
            column(j, h).wait_send()
    share.wait_send()


def fetch_rows(ids, table, seq):
    row = table.shape[1:]
    dma = pltpu.SemaphoreType.DMA
    vmem = pl.BlockSpec(memory_space=pltpu.VMEM)
    return pl.pallas_call(
        rows_kernel,
        out_shape=jax.ShapeDtypeStruct((seq,) + row, table.dtype),
        in_specs=[pl.BlockSpec(memory_space=pltpu.SMEM), vmem],
        out_specs=vmem,
        scratch_shapes=[pltpu.VMEM((2 * table.shape[0],) + row, table.dtype), pltpu.VMEM((4, seq) + row, table.dtype), pltpu.VMEM((12, seq) + row, table.dtype),
                        pltpu.VMEM((3, seq) + row, table.dtype), dma, dma, dma, dma((3, X_CHUNKS)), dma((3, X_CHUNKS)), dma((12, X_CHUNKS)), dma((12, X_CHUNKS))],
        compiler_params=pltpu.CompilerParams(collective_id=3, has_side_effects=True, vmem_limit_bytes=48 * 1024 * 1024),
        name='fetch_rows',
    )(ids, table)


N_ACC = 4
DX_CHUNKS = 4


def add_kernel(keys, starts, counts, base_ref, *refs):
    rows = refs[:DX_CHUNKS]
    out = refs[DX_CHUNKS]
    accs = refs[DX_CHUNKS + 1:DX_CHUNKS + 1 + N_ACC]
    buf, sem = refs[DX_CHUNKS + 1 + N_ACC:]
    n_out, width = out.shape
    seq = buf.shape[1] // SUBL
    part = buf.shape[1] // DX_CHUNKS
    base = base_ref[0]

    def load(i, h):
        slot = lax.rem(i, 2)
        return pltpu.make_async_copy(rows[h].at[i], buf.at[slot, pl.ds(h * part, part)], sem.at[slot, h])

    for h in range(DX_CHUNKS):
        load(0, h).start()

    @pl.loop(0, n_out)
    def _(r):
        for acc in accs:
            acc[pl.ds(pl.multiple_of(r * SUBL, SUBL), SUBL), :] = jnp.zeros((SUBL, LANES), jnp.float32)

    def add_row(i, k, acc):
        key = keys[i * seq + k]
        row = pl.multiple_of((lax.shift_right_logical(key, 9) - base) * SUBL, SUBL)
        src = pl.multiple_of(jnp.bitwise_and(key, 511) * SUBL, SUBL)
        acc[pl.ds(row, SUBL), :] += buf[lax.rem(i, 2), pl.ds(src, SUBL), :]

    @pl.loop(0, N_DEV)
    def _(i):
        @pl.when(i + 1 < N_DEV)
        def _():
            for h in range(DX_CHUNKS):
                load(i + 1, h).start()
        for h in range(DX_CHUNKS):
            load(i, h).wait()
        start = starts[i]
        count = counts[i]
        full = lax.div(count, 8)

        @pl.loop(0, full)
        def _(t):
            for u in range(8):
                add_row(i, start + t * 8 + u, accs[u % N_ACC])

        @pl.loop(full * 8, count)
        def _(k):
            add_row(i, start + k, accs[0])

    @pl.loop(0, n_out // SUBL)
    def _(r):
        for j in range(SUBL):
            lanes = min(LANES, width - j * LANES)
            value = accs[0][pl.ds(r * (SUBL * SUBL) + j, SUBL, stride=SUBL), :]
            for acc in accs[1:]:
                value = value + acc[pl.ds(r * (SUBL * SUBL) + j, SUBL, stride=SUBL), :]
            out[pl.ds(pl.multiple_of(r * SUBL, SUBL), SUBL), pl.ds(j * LANES, lanes)] = value[:, :lanes]


def add_rows(keys, starts, counts, base, rows, n_out, width):
    smem = pl.BlockSpec(memory_space=pltpu.SMEM)
    seq_rows = DX_CHUNKS * rows[0].shape[1]
    return pl.pallas_call(
        add_kernel,
        out_shape=jax.ShapeDtypeStruct((n_out, width), jnp.float32),
        in_specs=[smem] * 4 + [pl.BlockSpec(memory_space=pl.ANY)] * DX_CHUNKS,
        out_specs=pl.BlockSpec(memory_space=pltpu.VMEM),
        scratch_shapes=[pltpu.VMEM((n_out * SUBL, LANES), jnp.float32)] * N_ACC + [
            pltpu.VMEM((2, seq_rows, LANES), jnp.float32), pltpu.SemaphoreType.DMA((2, DX_CHUNKS))],
        compiler_params=pltpu.CompilerParams(vmem_limit_bytes=VMEM_BYTES),
        name='add_rows',
    )(keys, starts, counts, base, *rows)


def rope_tables(positions, head_dim):
    half_dim = head_dim // 2
    inv_freq = jnp.exp(jnp.arange(half_dim, dtype=jnp.float32) * (-2.0 * math.log(ROPE_THETA) / head_dim))
    angles = positions.astype(jnp.float32)[:, None] * inv_freq
    return jnp.cos(angles), jnp.sin(angles)


def rotate(values, cos_t, sin_t):
    half_dim = values.shape[-1] // 2
    lead_half = values[..., :half_dim]
    tail_half = values[..., half_dim:]
    return jnp.concatenate([lead_half * cos_t - tail_half * sin_t, tail_half * cos_t + lead_half * sin_t], axis=-1)


def norm_fwd(values):
    values_f = values.astype(jnp.float32)
    inv_rms = lax.rsqrt(jnp.mean(values_f * values_f, axis=-1, keepdims=True) + NORM_EPS)
    return values_f * inv_rms, inv_rms


def norm_bwd(grad_out, normed, inv_rms, norm_gain):
    grad_normed = grad_out * norm_gain.astype(jnp.float32)
    mean_term = jnp.mean(grad_normed * normed, axis=-1, keepdims=True)
    return inv_rms * (grad_normed - normed * mean_term)


def attn_fwd(q_rot, k_rot, v_raw):
    seq_len = q_rot.shape[0]
    attn_scale = q_rot.shape[-1] ** -0.5
    scores = jnp.einsum('qgrh,kgh->grqk', q_rot, k_rot, preferred_element_type=jnp.float32) * attn_scale
    causal = lax.broadcasted_iota(jnp.int32, (seq_len, seq_len), 0) >= lax.broadcasted_iota(jnp.int32, (seq_len, seq_len), 1)
    attn_probs = jax.nn.softmax(jnp.where(causal, scores, -1e30), axis=-1)
    attn_heads = jnp.einsum('grqk,kgh->qgrh', attn_probs.astype(jnp.bfloat16), v_raw, preferred_element_type=jnp.float32)
    return attn_heads.astype(jnp.bfloat16), attn_probs


def attn_bwd(grad_b, q_rot, k_rot, v_raw, attn_probs):
    attn_scale = q_rot.shape[-1] ** -0.5
    probs_b = attn_probs.astype(jnp.bfloat16)
    grad_probs = jnp.einsum('qgrh,kgh->grqk', grad_b, v_raw, preferred_element_type=jnp.float32)
    grad_v = jnp.einsum('grqk,qgrh->kgh', probs_b, grad_b, preferred_element_type=jnp.float32)
    grad_scores = attn_probs * (grad_probs - jnp.sum(grad_probs * attn_probs, axis=-1, keepdims=True)) * attn_scale
    scores_b = grad_scores.astype(jnp.bfloat16)
    grad_q = jnp.einsum('grqk,kgh->qgrh', scores_b, k_rot, preferred_element_type=jnp.float32)
    grad_k = jnp.einsum('grqk,qgrh->kgh', scores_b, q_rot, preferred_element_type=jnp.float32)
    return grad_q, grad_k, grad_v


def dot_f32(lhs, rhs):
    return jnp.dot(lhs, rhs, preferred_element_type=jnp.float32)


def dot_t(lhs, rhs):
    return lax.dot_general(lhs, rhs, (((0,), (0,)), ((), ())), preferred_element_type=jnp.float32)


def dot_nt(lhs, rhs):
    return lax.dot_general(lhs, rhs, (((1,), (1,)), ((), ())), preferred_element_type=jnp.float32)


def pad_rows(shard, rows):
    return jnp.pad(shard, ((0, rows - shard.shape[0]), (0, 0)))


def solution(mesh):
    row_spec = P(AXIS_NAME, None)
    vec_spec = P(AXIS_NAME)
    full_spec = P(None)
    batch_spec = P(AXIS_NAME, None, None)
    weight_specs = (vec_spec, row_spec, row_spec, row_spec, full_spec, full_spec, row_spec, vec_spec, row_spec, row_spec, row_spec)

    def device_step(tokens, positions, table_shard, attn_norm_s, w_query, w_key, w_value, q_norm, k_norm, w_out, mlp_norm_s, w_gate, w_up, w_down, dy_out):
        me = lax.axis_index(AXIS_NAME)
        seq = tokens.shape[1]
        rows_local, dim = table_shard.shape
        part = dim // N_DEV
        part_p = -(-part // 16) * 16
        dim_p = part_p * N_DEV
        head_dim = q_norm.shape[0]
        n_q = w_query.shape[1]
        n_kv = w_key.shape[1]
        kv_heads = n_kv // head_dim
        q_per_kv = n_q // n_kv

        ids = tokens[0]
        order = jnp.arange(seq, dtype=jnp.int32)
        keys = ids * seq + order
        rank = jnp.sum((keys[None, :] < keys[:, None]).astype(jnp.int32), axis=1)
        sorted_keys = jnp.sum(jnp.where(rank[None, :] == order[:, None], keys[None, :], 0), axis=1)
        all_keys = gather_ids(jnp.concatenate([ids, sorted_keys]).reshape(2 * seq // LANES, LANES)).reshape(N_DEV, 2, seq)
        all_ids = all_keys[:, 0]
        all_keys = all_keys[:, 1]
        chip_ids = (all_ids - me // NC * (NC * rows_local)).reshape(-1)
        width_p = SUBL * LANES
        table_rows = jnp.pad(table_shard, ((0, 0), (0, width_p - dim))).reshape(rows_local, SUBL, LANES)
        x_emb = fetch_rows(chip_ids, table_rows, seq).reshape(seq, width_p)[:, :dim].astype(jnp.float32)
        low = me * (rows_local * seq)
        my_starts = jnp.sum((all_keys < low).astype(jnp.int32), axis=1)
        my_counts = jnp.sum((all_keys < low + rows_local * seq).astype(jnp.int32), axis=1) - my_starts

        norm_pad = ((0, 0), (0, LANES - part))
        gains = jnp.concatenate([jnp.pad(attn_norm_s[None], norm_pad), jnp.pad(mlp_norm_s[None], norm_pad), jnp.zeros((14, LANES), attn_norm_s.dtype)], axis=0)
        w_qkv = jnp.concatenate([w_query, w_key, w_value], axis=1)
        blocks = [gains, pad_rows(w_qkv, part_p), pad_rows(w_out, part_p), pad_rows(w_gate, part_p), pad_rows(w_up, part_p), w_down]
        gains_all, w_qkv_p, w_out_p, w_gate_p, w_up_p, w_down_f = gather_blocks(blocks, 1, 'gather_weights')
        attn_norm = gains_all[:, 0, :part].reshape(dim)
        mlp_norm = gains_all[:, 1, :part].reshape(dim)
        w_qkv_p, w_out_p, w_gate_p, w_up_p, w_down_f = (w.reshape(-1, w.shape[-1]) for w in (w_qkv_p, w_out_p, w_gate_p, w_up_p, w_down_f))

        wide_pos = jnp.arange(dim_p, dtype=jnp.int32)
        dim_pos = jnp.arange(dim, dtype=jnp.int32)
        spread = (wide_pos[None, :] == (dim_pos // part * part_p + dim_pos % part)[:, None]).astype(jnp.bfloat16)

        def widen(values):
            return dot_f32(values, spread).astype(jnp.bfloat16)

        def narrow(values):
            return values.reshape(seq, N_DEV, part_p)[:, :, :part].reshape(seq, dim)

        cos_t, sin_t = rope_tables(positions[0], head_dim)
        cos_q, sin_q = cos_t[:, None, None, :], sin_t[:, None, None, :]
        cos_k, sin_k = cos_t[:, None, :], sin_t[:, None, :]
        normed1, norm1_inv = norm_fwd(x_emb)
        attn_in = widen((normed1 * attn_norm.astype(jnp.float32)).astype(jnp.bfloat16))
        qkv = dot_f32(attn_in, w_qkv_p).astype(jnp.bfloat16)
        q_raw = qkv[:, :n_q].reshape(seq, kv_heads, q_per_kv, head_dim)
        k_raw = qkv[:, n_q:n_q + n_kv].reshape(seq, kv_heads, head_dim)
        v_raw = qkv[:, n_q + n_kv:].reshape(seq, kv_heads, head_dim)
        q_normed, q_inv = norm_fwd(q_raw)
        k_normed, k_inv = norm_fwd(k_raw)
        q_rot = rotate(q_normed * q_norm.astype(jnp.float32), cos_q, sin_q).astype(jnp.bfloat16)
        k_rot = rotate(k_normed * k_norm.astype(jnp.float32), cos_k, sin_k).astype(jnp.bfloat16)
        attn_heads, attn_probs = attn_fwd(q_rot, k_rot, v_raw)
        attn_flat = widen(attn_heads.reshape(seq, n_q))
        hidden = (x_emb + dot_f32(attn_flat, w_out_p)).astype(jnp.bfloat16)
        normed2, norm2_inv = norm_fwd(hidden)
        mlp_in = widen((normed2 * mlp_norm.astype(jnp.float32)).astype(jnp.bfloat16))
        gate_pre = dot_f32(mlp_in, w_gate_p)
        up_proj = dot_f32(mlp_in, w_up_p)
        mlp_act = (jax.nn.silu(gate_pre) * up_proj).astype(jnp.bfloat16)
        layer_out = (hidden.astype(jnp.float32) + dot_f32(mlp_act, w_down_f)).astype(jnp.bfloat16)

        dy = dy_out[0]
        grad_w_down = dot_t(mlp_act, dy)
        grad_act = dot_nt(dy, w_down_f)
        gate_sig = jax.nn.sigmoid(gate_pre)
        grad_gate = (grad_act * up_proj * gate_sig * (1.0 + gate_pre * (1.0 - gate_sig))).astype(jnp.bfloat16)
        grad_up = (grad_act * gate_pre * gate_sig).astype(jnp.bfloat16)
        grad_w_gate = dot_t(mlp_in, grad_gate)
        grad_w_up = dot_t(mlp_in, grad_up)
        grad_mlp_in = narrow(dot_nt(grad_gate, w_gate_p) + dot_nt(grad_up, w_up_p))
        grad_mlp_norm = jnp.sum(grad_mlp_in * normed2, axis=0)
        grad_hidden = dy.astype(jnp.float32) + norm_bwd(grad_mlp_in, normed2, norm2_inv, mlp_norm)
        hidden_b = grad_hidden.astype(jnp.bfloat16)
        grad_w_out = dot_t(attn_flat, hidden_b)
        grad_heads = dot_nt(dot_nt(hidden_b, w_out_p).astype(jnp.bfloat16), spread).astype(jnp.bfloat16).reshape(q_rot.shape)
        grad_q, grad_k, grad_v = attn_bwd(grad_heads, q_rot, k_rot, v_raw, attn_probs)
        grad_qt = rotate(grad_q, cos_q, -sin_q)
        grad_kt = rotate(grad_k, cos_k, -sin_k)
        grad_q_norm = jnp.sum(grad_qt * q_normed, axis=(0, 1, 2))
        grad_k_norm = jnp.sum(grad_kt * k_normed, axis=(0, 1))
        grad_q_raw = norm_bwd(grad_qt, q_normed, q_inv, q_norm).astype(jnp.bfloat16).reshape(seq, n_q)
        grad_k_raw = norm_bwd(grad_kt, k_normed, k_inv, k_norm).astype(jnp.bfloat16).reshape(seq, n_kv)
        grad_v_raw = grad_v.astype(jnp.bfloat16).reshape(seq, n_kv)
        grad_qkv = jnp.concatenate([grad_q_raw, grad_k_raw, grad_v_raw], axis=1)
        grad_attn_in = narrow(dot_nt(grad_qkv, w_qkv_p))
        grad_x_emb = grad_hidden + norm_bwd(grad_attn_in, normed1, norm1_inv, attn_norm)
        dx_rows = jnp.pad(grad_x_emb, ((0, 0), (0, width_p - dim))).reshape(DX_CHUNKS, seq * SUBL // DX_CHUNKS, LANES)
        dx_all = gather_blocks([dx_rows[h] for h in range(DX_CHUNKS)], 4, 'gather_dx')

        grad_attn_norm = jnp.sum(grad_attn_in * normed1, axis=0)
        grad_w_qkv = dot_t(attn_in, grad_qkv)
        small = jnp.stack([jnp.pad(grad_attn_norm.reshape(N_DEV, part), norm_pad), jnp.pad(grad_mlp_norm.reshape(N_DEV, part), norm_pad),
                           jnp.broadcast_to(jnp.concatenate([grad_q_norm, grad_k_norm])[None], (N_DEV, 2 * head_dim))], axis=1)
        small = jnp.pad(small, ((0, 0), (0, SUBL - 3), (0, 0)))
        parts = [small] + [g.reshape(N_DEV, -1, g.shape[-1]) for g in (grad_w_qkv, grad_w_out, grad_w_gate, grad_w_up, grad_w_down)]
        small_s, qkv_s, out_s, gate_s, up_s, down_s = scatter_grads(parts)
        d_table = add_rows(all_keys.reshape(-1), my_starts, my_counts, (me * rows_local).reshape(1), dx_all, rows_local, dim)
        return (layer_out[None], d_table, small_s[0, :part], qkv_s[:part, :n_q], qkv_s[:part, n_q:n_q + n_kv], qkv_s[:part, n_q + n_kv:],
                small_s[2, :head_dim], small_s[2, head_dim:], out_s[:part], small_s[1, :part], gate_s[:part], up_s[:part], down_s)

    return jax.shard_map(device_step, mesh=mesh, in_specs=(row_spec, row_spec, row_spec) + weight_specs + (batch_spec,), out_specs=(batch_spec, row_spec) + weight_specs, check_vma=False)
```

time: 1620 us -> 1120 us (0.69)
  the two profiles are of different devices: /device:TPU:0 before, /device:TPU:23 now
where the time goes in v1:
time: 1120 us; the launch traced here: 1110 us
  Pallas kernels  831 us (74%)
  matrix products  157 us (14%)
  local copies, waits for them, and re-layouts  79.7 us (7%)
  other arithmetic  41 us (4%)
    pallas_call x2, Pallas kernels, gather_blocks(): pl.pallas_call(functools.partial(weights_kernel, n_arr), out_shape=out_sh...  440 us
    pallas_call x1, Pallas kernels, scatter_grads(): pl.pallas_call(functools.partial(grads_kernel, n_arr), out_shape=tuple((j...  186 us
    pallas_call x1, Pallas kernels, fetch_rows(): pl.pallas_call(rows_kernel, out_shape=jax.ShapeDtypeStruct((seq,) + row,...  148 us
    pallas_call x1, Pallas kernels, add_rows(): pl.pallas_call(add_kernel, out_shape=jax.ShapeDtypeStruct((n_out, width),...  46 us
    unnamed x167, local copies, waits for them, and re-layouts  37.9 us
    dot_general x8, matrix products, dot_f32(): return jnp.dot(lhs, rhs, preferred_element_type=jnp.float32)  30.9 us
    dot_general x5, matrix products, dot_t(): lax.dot_general(lhs, rhs, (((0,), (0,)), ((), ())), preferred_element_typ...  26.5 us
    dot_general x1, matrix products, attn_bwd(): jnp.einsum('grqk,kgh->qgrh', scores_b, k_rot, preferred_element_type=jnp....  22.8 us

profile of v1, /device:TPU:23, one launch (start us, length us, event | category | flops | bytes accessed | tf_op | source)
XLA Modules:
  0.0 1110.8 jit_solution(5013081428364028480)
XLA Ops:
  12.7 10.6 gather_ids.1
  37.8 148.4 %fetch_rows.1 = bf16[512,8,128]{2,1,0:T(8,128)(2,1)S(1)} custom-call(s32[16384]{0:T(1024)S(1)} %bitcast.218, bf16[1536,8,128]{2,1,0:T(8,128)(2,1)S(1)} %copy.87.table), custom_call_target="tpu_custom_call" | custom-call | tf_op jit(solution)/shard_map/fetch_rows/pallas_call | solution.py:398
  190.0 108.6 %gather_weights.1 = (bf16[32,16,128]{2,1,0:T(8,128)(2,1)S(1)}, bf16[32,32,1600]{2,1,0:T(8,128)(2,1)S(1)}, bf16[32,32,960]{2,1,0:T(8,128)(2,1)S(1)}, bf16[32,32,2...) custom-call(bf16[16,128]{1,0:T(8,128)(2,1)S(1)} %fusion.115.refs_0_, ...), custom_call_target="tpu_custom_call" | custom-call | tf_op jit(solution)/shard_map/gather_weights/pallas_call | solution.py:171
  318.5 5.0 fusion.85
  323.5 12.0 %fusion.133 = (f32[5,3,512]{2,1,0:T(4,128)S(1)}, f32[5,3,512,512]{2,3,1,0:T(8,128)}) fusion(pred[512,512]{0,1:T(8,128)(4,1)} %iota_compare_fusion.13, bf16[512,5,3,32]{0,3,2,1:T(8,128)(2,1)S(1)} %get-tuple-element.97, bf16[512,5,3,32]{0,3,2,1:T(8,128)(2,1)S(1)} %get-tuple-element.96, bf16[512,5,32]{0,2,1:T(8,128)(2,1)} %get-tuple-element.113, ...), kind=kOutput, calls=%fused_computation.215 | convolution fusion | flops 521667072 | bytes 17332224 | tf_op jit(solution)/shard_map/sub | solution.py:519
  335.6 7.0 fusion.69
  349.9 11.0 fusion.20
  360.9 7.9 fusion.73
  368.9 7.2 fusion.12
  388.8 4.8 copy.74
  402.5 8.9 fusion.78
  414.7 5.5 fusion.83.refs_5_
  420.3 5.5 fusion.138
  425.8 5.6 fusion.137
  431.5 7.8 fusion.136
  439.3 21.7 %fusion.74 = f32[512,5,64]{0,2,1:T(8,128)S(1)} fusion(f32[5,512,512,3]{2,1,3,0:T(8,128)} %fusion.136, bf16[512,5,3,32]{0,3,2,1:T(8,128)(2,1)} %copy-done.41, bf16[512,5,3,32]{0,3,2,1:T(8,128)(2,1)} %copy-done.40, f32[5,3,512,512]{2,3,1,0:T(8,128)} %get-tuple-element.130, f32[5,3,512]{2,1,0:T(4,128)S(1)} %copy-done.72), kind=kOutput, calls=%fused_computation.106 | convolution fusion | flops 532815872 | bytes 33126400 | tf_op jit(solution)/shard_map/grqk,qgrh->kgh/dot_general | solution.py:532
  461.0 22.8 %fusion.65 = f32[512,5,3,64]{0,3,2,1:T(8,128)} fusion(f32[5,512,512,3]{2,1,3,0:T(8,128)} %fusion.136, bf16[512,5,32]{0,2,1:T(8,128)(2,1)S(1)} %copy-done.48, bf16[512,5,32]{0,2,1:T(8,128)(2,1)S(1)} %copy-done.47, f32[5,3,512,512]{2,3,1,0:T(8,128)} %get-tuple-element.130, f32[5,3,512]{2,1,0:T(4,128)S(1)} %copy-done.72), kind=kOutput, calls=%fused_computation.97 | convolution fusion | flops 531505152 | bytes 33781760 | tf_op jit(solution)/shard_map/grqk,kgh->qgrh/dot_general | solution.py:531
  513.0 6.4 fusion.91
  519.4 186.3 %scatter_grads.1 = (f32[8,128]{1,0:T(8,128)}, f32[32,1600]{1,0:T(8,128)}, f32[32,960]{1,0:T(8,128)}, f32[32,2560]{1,0:T(8,128)}, f32[32,2560]{1,0:T(8,128)}, /*index=5*/f32[80,960]{1,0:T(8,128)}) custom-call(f32[32,8,128]{2,1,0:T(8,128)} %select_maximum_fusion.refs_0_, f32[32,32,1600]{2,1,0:T(8,128)} %bitcast.253, f32[32,32,960]{2,1,0:T(8,128)} %bitcast.239, ...), custom_call_target="tpu_custom_call" | custom-call | tf_op jit(solution)/shard_map/scatter_grads/pallas_call | solution.py:292
  712.6 331.1 %gather_dx.1 = (f32[32,1024,128]{2,1,0:T(8,128)S(1)}, f32[32,1024,128]{2,1,0:T(8,128)S(1)}, f32[32,1024,128]{2,1,0:T(8,128)}, f32[32,1024,128]{2,1,0:T(8,128)}) custom-call(f32[1024,128]{1,0:T(8,128)S(1)} %copy-done.3, f32[1024,128]{1,0:T(8,128)S(1)} %squeeze.33.refs_1_, f32[1024,128]{1,0:T(8,128)S(1)} %squeeze.34.refs_2_, f32[1024,128]{1,0:T(8,128)S(1)} %squeeze.35.refs_3_), custom_call_target="tpu_custom_call" | custom-call | tf_op jit(solution)/shard_map/gather_dx/pallas_call | solution.py:171
  1043.7 5.7 copy-done
  1049.4 5.7 copy-done.1
  1055.2 46.0 %add_rows.1 = f32[1536,960]{1,0:T(8,128)} custom-call(s32[16384]{0:T(1024)} %bitcast.262, s32[32]{0:T(128)} %copy-done.57, s32[32]{0:T(128)} %sub.83.counts, s32[1]{0:T(128)} %bitcast.27.base_ref, f32[32,1024,128]{2,1,0:T(8,128)} %copy-done, f32[32,1024,128]{2,1,0:T(8,128)} %copy-done.1, f32[32,1024,128]{2,1,0:T(8,128)} %get-tuple-element.37.refs_2_, ...), custom_call_target="tpu_custom_call" | custom-call | tf_op jit(solution)/shard_map/add_rows/pallas_call | solution.py:476
  1101.2 6.5 copy.75
  (268 shorter events, 120.4 us)
Async XLA Ops:
  26.1 7.9 copy-start.57
  189.9 120.5 %copy-start.53 = (f32[512]{0:T(512)}, f32[512]{0:T(512)S(1)}, u32[]{:S(2)}) copy-start(f32[512]{0:T(512)S(1)} %add_rsqrt_fusion.3) | copy-start | bytes 6148
  313.5 22.0 %copy-start.30 = (bf16[512,320]{0,1:T(8,128)(2,1)}, bf16[512,320]{0,1:T(8,128)(2,1)S(1)}, u32[]{:S(2)}) copy-start(bf16[512,320]{0,1:T(8,128)(2,1)S(1)} %get-tuple-element.109) | copy-start | bytes 983044
  335.5 7.0 copy-start.71
  346.9 13.9 %slice-start.6 = ((s8[5242880]{0:T(1024)(128)(4,1)}), s8[4194304]{0:T(1024)(128)(4,1)S(1)}, s32[]{:S(2)}) async-start(s8[5242880]{0:T(1024)(128)(4,1)} %bitcast.230), calls=%async_computation.6 | async-start | bytes 8388608
  349.9 11.0 copy-start.24
  349.9 11.0 slice-start.7
  368.8 7.2 copy-start.65
  402.5 8.9 copy-start.15
  402.5 8.9 copy-start.27
  414.7 5.6 copy-start.68
  414.7 5.6 copy-start.70
  425.8 5.7 copy-start.31
  431.5 7.8 copy-start.72
  439.3 21.7 %copy-start.47 = (bf16[512,5,32]{0,2,1:T(8,128)(2,1)S(1)}, bf16[512,5,32]{0,2,1:T(8,128)(2,1)}, u32[]{:S(2)}) copy-start(bf16[512,5,32]{0,2,1:T(8,128)(2,1)} %get-tuple-element.112) | copy-start | bytes 491524
  439.3 21.7 %copy-start.48 = (bf16[512,5,32]{0,2,1:T(8,128)(2,1)S(1)}, bf16[512,5,32]{0,2,1:T(8,128)(2,1)}, u32[]{:S(2)}) copy-start(bf16[512,5,32]{0,2,1:T(8,128)(2,1)} %get-tuple-element.113) | copy-start | bytes 491524
  461.0 22.8 %copy-start.29 = (f32[512,32]{0,1:T(8,128)S(1)}, f32[512,32]{0,1:T(8,128)}, u32[]{:S(2)}) copy-start(f32[512,32]{0,1:T(8,128)} %get-tuple-element.126) | copy-start | bytes 196612
  461.0 22.8 %copy-start.38 = (f32[512,32]{0,1:T(8,128)S(1)}, f32[512,32]{0,1:T(8,128)}, u32[]{:S(2)}) copy-start(f32[512,32]{0,1:T(8,128)} %get-tuple-element.124) | copy-start | bytes 196612
  1043.7 5.8 copy-start
  1049.4 5.7 copy-start.1
  1101.2 6.5 copy-start.49
  1101.2 7.2 copy-start.44
  1101.2 7.9 copy-start.43
  1101.2 8.6 copy-start.42
  (57 other events, 139.8 us)

commit v2 on v1

--- a/solution.py
+++ b/solution.py
@@ -86,97 +86,186 @@
     )(block)
 
 
-def weights_kernel(n_arr, *refs):
-    ins = refs[:n_arr]
-    outs = refs[n_arr:2 * n_arr]
-    loc_sem, z_send, z_recv, r_send, r_recv, p_send, p_recv = refs[2 * n_arr:]
+def blocks_kernel(n_a, n_b, stacked, *refs):
+    n_arr = n_a + n_b
+    if stacked:
+        ins = [refs[0].at[a] for a in range(n_arr)]
+        refs = refs[1:]
+    else:
+        ins = refs[:n_arr]
+        refs = refs[n_arr:]
+    outs = refs[:n_arr]
+    loc_sem, az_send, az_recv, ar_send, ar_recv, ap_send, ap_recv, bz_send, bz_recv, br_send, br_recv, bp_send, bp_recv = refs[n_arr:]
     me, z, q, c = my_coords()
     step_dir = 1 - 2 * c
     nxt = dev_id(z, wrap4(q + step_dir), c)
     mate = dev_id(z, q, 1 - c)
+    high = lax.div(z, 2)
+    inner = lax.div(wrap4(z + 1), 2)
     entry_barrier(z, q, c)
 
     def remote(src, dst, send, recv, target):
         return pltpu.make_async_remote_copy(src_ref=src, dst_ref=dst, send_sem=send, recv_sem=recv, device_id=(target,), device_id_type=MESH)
 
-    def block_at(j, s):
-        return dev_id(wrap4(z - j), wrap4(q - step_dir * s), c)
-
-    def source(a, j, s):
-        return ins[a] if (j, s) == (0, 0) else outs[a].at[block_at(j, s)]
-
-    def ring(a, j, s):
-        return remote(source(a, j, s), outs[a].at[block_at(j, s)], r_send.at[a, s, j], r_recv.at[a, s, j], nxt)
-
-    def ring_in(a, j, s):
-        dst = outs[a].at[block_at(j, s + 1)]
-        return remote(dst, dst, r_send.at[a, s, j], r_recv.at[a, s, j], nxt)
-
-    def pair(a, j, s):
-        return remote(source(a, j, s), outs[a].at[block_at(j, s)], p_send.at[a, s, j], p_recv.at[a, s, j], mate)
-
-    def pair_in(a, j, s):
-        dst = outs[a].at[dev_id(wrap4(z - j), wrap4(q + step_dir * s), 1 - c)]
-        return remote(dst, dst, p_send.at[a, s, j], p_recv.at[a, s, j], mate)
-
-    def column(a, k):
-        return remote(ins[a], outs[a].at[me], z_send.at[a, k - 1], z_recv.at[a, k - 1], dev_id(wrap4(z + k), q, c))
-
-    def column_in(a, k):
-        dst = outs[a].at[dev_id(wrap4(z - k), q, c)]
-        return remote(dst, dst, z_send.at[a, k - 1], z_recv.at[a, k - 1], dev_id(wrap4(z + k), q, c))
-
-    arrays = range(n_arr)
-    local = [pltpu.make_async_copy(ins[a], outs[a].at[me], loc_sem.at[a]) for a in arrays]
-    for a in arrays:
+    def source_z(t):
+        if t == 0:
+            return z
+        base = t - inner if t == 1 else t
+        return base + high * (3 - 2 * base)
+
+    def block_at(t, s):
+        return dev_id(source_z(t), wrap4(q - step_dir * s), c)
+
+    def spot(a, t, s):
+        return outs[a].at[block_at(t, s)]
+
+    def source(a, t, s):
+        return ins[a] if (t, s) == (0, 0) else spot(a, t, s)
+
+    def ring(a, t, s):
+        if a < n_a:
+            sems = ar_send.at[a, s, t], ar_recv.at[a, s, t]
+        else:
+            sems = br_send.at[a - n_a, s], br_recv.at[a - n_a, s]
+        return remote(source(a, t, s), spot(a, t, s), *sems, nxt)
+
+    def ring_in(a, t, s):
+        if a < n_a:
+            sems = ar_send.at[a, s, t], ar_recv.at[a, s, t]
+        else:
+            sems = br_send.at[a - n_a, s], br_recv.at[a - n_a, s]
+        return remote(spot(a, t, s + 1), spot(a, t, s + 1), *sems, nxt)
+
+    def pair_sems(a, t, s):
+        if a < n_a:
+            return ap_send.at[a, s, t], ap_recv.at[a, s, t]
+        return bp_send.at[a - n_a, s, t], bp_recv.at[a - n_a, s, t]
+
+    def pair(a, t, s):
+        return remote(source(a, t, s), spot(a, t, s), *pair_sems(a, t, s), mate)
+
+    def pair_in(a, t, s):
+        dst = outs[a].at[dev_id(source_z(t), wrap4(q + step_dir * s), 1 - c)]
+        return remote(dst, dst, *pair_sems(a, t, s), mate)
+
+    def column(a, t, s, up):
+        side = 0 if up else 1
+        if a < n_a:
+            sems = az_send.at[a, side, t], az_recv.at[a, source_z(t)]
+        else:
+            sems = bz_send.at[a - n_a, s, side, t], bz_recv.at[a - n_a, s, source_z(t)]
+        return remote(source(a, t, s), spot(a, t, s), *sems, dev_id(z + 1 if up else z - 1, q, c))
+
+    def column_in(a, t, s):
+        if a < n_a:
+            sems = az_send.at[a, 0, t], az_recv.at[a, source_z(t)]
+        else:
+            sems = bz_send.at[a - n_a, s, 0, t], bz_recv.at[a - n_a, s, source_z(t)]
+        return remote(spot(a, t, s), spot(a, t, s), *sems, mate)
+
+    def spread(a, t, s, act):
+        if t == 0:
+            ups, downs = z < NZ - 1, z > 0
+        else:
+            ups = jnp.logical_and(inner == 1, source_z(t) < z)
+            downs = jnp.logical_and(inner == 1, source_z(t) > z)
+
+        @pl.when(ups)
+        def _():
+            act(column(a, t, s, True))
+
+        @pl.when(downs)
+        def _():
+            act(column(a, t, s, False))
+
+    def launch(copy):
+        copy.start()
+
+    def settle(copy):
+        copy.wait_send()
+
+    first = range(n_a)
+    second = range(n_a, n_arr)
+    local = [pltpu.make_async_copy(ins[a], outs[a].at[me], loc_sem.at[a]) for a in range(n_arr)]
+    for a in list(second) + list(first):
         ring(a, 0, 0).start()
-    for k in (1, 3, 2):
-        for a in arrays:
-            column(a, k).start()
-    for a in arrays:
+    for a in range(n_arr):
+        spread(a, 0, 0, launch)
+    for a in range(n_arr):
         local[a].start()
         pair(a, 0, 0).start()
 
-    groups = [(0, 0)]
-    for pos, j in enumerate(J_GATHER):
-        groups += [(j, 1), (j, 2)]
-        if pos + 1 < NZ:
-            groups.append((J_GATHER[pos + 1], 0))
-        groups.append((j, 3))
-    for j, s in groups[1:]:
-        for a in arrays:
+    def ring_step(a, t, s):
+        ring_in(a, t, s - 1).wait_recv()
+        if s < 3:
+            ring(a, t, s).start()
+        pair(a, t, s).start()
+
+    groups = []
+    for t in range(NZ):
+        groups += [(t, 1), (t, 2)]
+        if t + 1 < NZ:
+            groups.append((t + 1, 0))
+        groups.append((t, 3))
+    later = [(t, s) for t in (1, 2, 3) for s in range(4)]
+    for t, s in groups:
+        for a in first:
             if s == 0:
-                column_in(a, j).wait_recv()
+                column_in(a, t, 0).wait_recv()
+                ring(a, t, 0).start()
+                spread(a, t, 0, launch)
+                pair(a, t, 0).start()
             else:
-                ring_in(a, j, s - 1).wait_recv()
-            if s < 3:
-                ring(a, j, s).start()
-            pair(a, j, s).start()
-    for a in arrays:
+                ring_step(a, t, s)
+        for a in second:
+            if t == 0 and s > 0:
+                ring_step(a, 0, s)
+                spread(a, 0, s, launch)
+            if (t, s) in ((0, 1), (0, 2)) or not later:
+                continue
+            tb, sb = later[0]
+            if tb == 1 and sb == 3 and (t, s) == (1, 0):
+                continue
+            column_in(a, tb, sb).wait_recv()
+            spread(a, tb, sb, launch)
+            pair(a, tb, sb).start()
+        if (t, s) not in ((0, 1), (0, 2)) and later:
+            later.pop(0)
+    for tb, sb in later:
+        for a in second:
+            column_in(a, tb, sb).wait_recv()
+            spread(a, tb, sb, launch)
+            pair(a, tb, sb).start()
+    for a in range(n_arr):
         local[a].wait()
-        for j in range(NZ):
+        for t in range(NZ):
             for s in range(4):
-                pair_in(a, j, s).wait_recv()
-                pair(a, j, s).wait_send()
-                if s < 3:
-                    ring(a, j, s).wait_send()
-        for k in (1, 2, 3):
-            column(a, k).wait_send()
-
-
-def gather_blocks(blocks, collective_id, name):
-    n_arr = len(blocks)
-    out_shape = tuple(jax.ShapeDtypeStruct((N_DEV,) + b.shape, b.dtype) for b in blocks)
+                pair_in(a, t, s).wait_recv()
+                pair(a, t, s).wait_send()
+                if s < 3 and (a < n_a or t == 0):
+                    ring(a, t, s).wait_send()
+                if s == 0 or a >= n_a:
+                    spread(a, t, s, settle)
+
+
+def gather_blocks(blocks, n_b, collective_id, name):
+    stacked = not isinstance(blocks, list)
+    n_arr = blocks.shape[0] if stacked else len(blocks)
+    n_a = n_arr - n_b
+    n_b1 = max(n_b, 1)
+    out_shape = tuple(jax.ShapeDtypeStruct((N_DEV,) + blocks[a].shape, blocks[a].dtype) for a in range(n_arr))
     dma = pltpu.SemaphoreType.DMA
+    operands = [blocks] if stacked else blocks
     return pl.pallas_call(
-        functools.partial(weights_kernel, n_arr),
+        functools.partial(blocks_kernel, n_a, n_b, stacked),
         out_shape=out_shape,
-        in_specs=[pl.BlockSpec(memory_space=pltpu.VMEM)] * n_arr,
-        out_specs=tuple(pl.BlockSpec(memory_space=pl.ANY) for _ in blocks),
-        scratch_shapes=[dma((n_arr,)), dma((n_arr, 3)), dma((n_arr, 3)), dma((n_arr, 3, 4)), dma((n_arr, 3, 4)), dma((n_arr, 4, 4)), dma((n_arr, 4, 4))],
+        in_specs=[pl.BlockSpec(memory_space=pltpu.VMEM)] * len(operands),
+        out_specs=tuple(pl.BlockSpec(memory_space=pltpu.HBM) for _ in range(n_arr)),
+        scratch_shapes=[dma((n_arr,)), dma((n_a, 2, 4)), dma((n_a, 4)), dma((n_a, 3, 4)), dma((n_a, 3, 4)), dma((n_a, 4, 4)), dma((n_a, 4, 4)),
+                        dma((n_b1, 4, 2, 4)), dma((n_b1, 4, 4)), dma((n_b1, 3)), dma((n_b1, 3)), dma((n_b1, 4, 4)), dma((n_b1, 4, 4))],
         compiler_params=pltpu.CompilerParams(collective_id=collective_id, has_side_effects=True, vmem_limit_bytes=8 * 1024 * 1024),
         name=name,
-    )(*blocks)
+    )(*operands)
 
 
 def grads_kernel(n_arr, *refs):
@@ -292,7 +381,7 @@
     return pl.pallas_call(
         functools.partial(grads_kernel, n_arr),
         out_shape=tuple(jax.ShapeDtypeStruct(s, jnp.float32) for s in shapes),
-        in_specs=[pl.BlockSpec(memory_space=pl.ANY)] * n_arr,
+        in_specs=[pl.BlockSpec(memory_space=pltpu.HBM)] * n_arr,
         out_specs=tuple(pl.BlockSpec(memory_space=pltpu.VMEM) for _ in parts),
         scratch_shapes=bufs(2) + bufs(16) + bufs(12) + bufs(3) + [
             dma((n_arr, 2)), dma((n_arr, 3)), dma((n_arr, 3)), dma((n_arr, 12)), dma((n_arr, 12)), dma((n_arr, 16)), dma((n_arr, 16))],
@@ -411,22 +500,74 @@
 DX_CHUNKS = 4
 
 
-def add_kernel(keys, starts, counts, base_ref, *refs):
+def pack_kernel(rank, dx, out, tmp):
+    seq, width = dx.shape
+    part = seq // DX_CHUNKS
+
+    @pl.loop(0, seq // SUBL)
+    def _(r):
+        here = pl.ds(pl.multiple_of(r * SUBL, SUBL), SUBL)
+        for j in range(SUBL):
+            lanes = min(LANES, width - j * LANES)
+            value = dx[here, pl.ds(j * LANES, lanes)]
+            if lanes < LANES:
+                value = jnp.concatenate([value, jnp.zeros((SUBL, LANES - lanes), value.dtype)], axis=1)
+            tmp[pl.ds(r * (SUBL * SUBL) + j, SUBL, stride=SUBL), :] = value
+
+    @pl.loop(0, seq // SUBL)
+    def _(r):
+        for u in range(SUBL):
+            i = r * SUBL + u
+            place = rank[i]
+            row = pl.multiple_of(lax.rem(place, part) * SUBL, SUBL)
+            out[lax.div(place, part), pl.ds(row, SUBL), :] = tmp[pl.ds(pl.multiple_of(i * SUBL, SUBL), SUBL), :]
+
+
+def pack_rows(rank, dx):
+    seq = dx.shape[0]
+    vmem = pl.BlockSpec(memory_space=pltpu.VMEM)
+    return pl.pallas_call(
+        pack_kernel,
+        out_shape=jax.ShapeDtypeStruct((DX_CHUNKS, seq * SUBL // DX_CHUNKS, LANES), dx.dtype),
+        in_specs=[pl.BlockSpec(memory_space=pltpu.SMEM), vmem],
+        out_specs=vmem,
+        scratch_shapes=[pltpu.VMEM((seq * SUBL, LANES), dx.dtype)],
+        compiler_params=pltpu.CompilerParams(vmem_limit_bytes=16 * 1024 * 1024),
+        name='pack_rows',
+    )(rank, dx)
+
+
+OUT_ROWS = 128
+
+
+def add_kernel(ids, starts, counts, *refs):
     rows = refs[:DX_CHUNKS]
     out = refs[DX_CHUNKS]
     accs = refs[DX_CHUNKS + 1:DX_CHUNKS + 1 + N_ACC]
-    buf, sem = refs[DX_CHUNKS + 1 + N_ACC:]
+    buf, sem, stage, stage_sem = refs[DX_CHUNKS + 1 + N_ACC:]
     n_out, width = out.shape
     seq = buf.shape[1] // SUBL
-    part = buf.shape[1] // DX_CHUNKS
-    base = base_ref[0]
+    part = seq // DX_CHUNKS
 
     def load(i, h):
-        slot = lax.rem(i, 2)
-        return pltpu.make_async_copy(rows[h].at[i], buf.at[slot, pl.ds(h * part, part)], sem.at[slot, h])
-
-    for h in range(DX_CHUNKS):
-        load(0, h).start()
+        slot = lax.rem(i, 3)
+        return pltpu.make_async_copy(rows[h].at[i], buf.at[slot, pl.ds(h * part * SUBL, part * SUBL)], sem.at[slot, h])
+
+    def each_load(i, act):
+        low, high = starts[i], starts[i] + counts[i]
+        for h in range(DX_CHUNKS):
+            @pl.when(jnp.logical_and(low < (h + 1) * part, jnp.logical_and(high > h * part, counts[i] > 0)))
+            def _():
+                act(load(i, h))
+
+    def launch(copy):
+        copy.start()
+
+    def settle(copy):
+        copy.wait()
+
+    each_load(0, launch)
+    each_load(1, launch)
 
     @pl.loop(0, n_out)
     def _(r):
@@ -434,19 +575,15 @@
             acc[pl.ds(pl.multiple_of(r * SUBL, SUBL), SUBL), :] = jnp.zeros((SUBL, LANES), jnp.float32)
 
     def add_row(i, k, acc):
-        key = keys[i * seq + k]
-        row = pl.multiple_of((lax.shift_right_logical(key, 9) - base) * SUBL, SUBL)
-        src = pl.multiple_of(jnp.bitwise_and(key, 511) * SUBL, SUBL)
-        acc[pl.ds(row, SUBL), :] += buf[lax.rem(i, 2), pl.ds(src, SUBL), :]
+        row = pl.multiple_of(ids[i * seq + k] * SUBL, SUBL)
+        acc[pl.ds(row, SUBL), :] += buf[lax.rem(i, 3), pl.ds(pl.multiple_of(k * SUBL, SUBL), SUBL), :]
 
     @pl.loop(0, N_DEV)
     def _(i):
-        @pl.when(i + 1 < N_DEV)
+        @pl.when(i + 2 < N_DEV)
         def _():
-            for h in range(DX_CHUNKS):
-                load(i + 1, h).start()
-        for h in range(DX_CHUNKS):
-            load(i, h).wait()
+            each_load(i + 2, launch)
+        each_load(i, settle)
         start = starts[i]
         count = counts[i]
         full = lax.div(count, 8)
@@ -460,29 +597,45 @@
         def _(k):
             add_row(i, start + k, accs[0])
 
-    @pl.loop(0, n_out // SUBL)
-    def _(r):
-        for j in range(SUBL):
-            lanes = min(LANES, width - j * LANES)
-            value = accs[0][pl.ds(r * (SUBL * SUBL) + j, SUBL, stride=SUBL), :]
-            for acc in accs[1:]:
-                value = value + acc[pl.ds(r * (SUBL * SUBL) + j, SUBL, stride=SUBL), :]
-            out[pl.ds(pl.multiple_of(r * SUBL, SUBL), SUBL), pl.ds(j * LANES, lanes)] = value[:, :lanes]
-
-
-def add_rows(keys, starts, counts, base, rows, n_out, width):
+    def store(m):
+        here = pl.ds(pl.multiple_of(m * OUT_ROWS, OUT_ROWS), OUT_ROWS)
+        return pltpu.make_async_copy(stage.at[lax.rem(m, 2)], out.at[here], stage_sem.at[lax.rem(m, 2)])
+    n_store = n_out // OUT_ROWS
+
+    @pl.loop(0, n_store)
+    def _(m):
+        @pl.when(m >= 2)
+        def _():
+            store(m - 2).wait()
+
+        @pl.loop(0, OUT_ROWS // SUBL)
+        def _(r):
+            for j in range(SUBL):
+                lanes = min(LANES, width - j * LANES)
+                here = pl.ds(m * (OUT_ROWS * SUBL) + r * (SUBL * SUBL) + j, SUBL, stride=SUBL)
+                value = accs[0][here, :]
+                for acc in accs[1:]:
+                    value = value + acc[here, :]
+                stage[lax.rem(m, 2), pl.ds(pl.multiple_of(r * SUBL, SUBL), SUBL), pl.ds(j * LANES, lanes)] = value[:, :lanes]
+        store(m).start()
+    for m in (n_store - 2, n_store - 1):
+        store(m).wait()
+
+
+def add_rows(ids, starts, counts, rows, n_out, width):
     smem = pl.BlockSpec(memory_space=pltpu.SMEM)
     seq_rows = DX_CHUNKS * rows[0].shape[1]
     return pl.pallas_call(
         add_kernel,
         out_shape=jax.ShapeDtypeStruct((n_out, width), jnp.float32),
-        in_specs=[smem] * 4 + [pl.BlockSpec(memory_space=pl.ANY)] * DX_CHUNKS,
-        out_specs=pl.BlockSpec(memory_space=pltpu.VMEM),
+        in_specs=[smem] * 3 + [pl.BlockSpec(memory_space=pltpu.HBM)] * DX_CHUNKS,
+        out_specs=pl.BlockSpec(memory_space=pltpu.HBM),
         scratch_shapes=[pltpu.VMEM((n_out * SUBL, LANES), jnp.float32)] * N_ACC + [
-            pltpu.VMEM((2, seq_rows, LANES), jnp.float32), pltpu.SemaphoreType.DMA((2, DX_CHUNKS))],
+            pltpu.VMEM((3, seq_rows, LANES), jnp.float32), pltpu.SemaphoreType.DMA((3, DX_CHUNKS)),
+            pltpu.VMEM((2, OUT_ROWS, width), jnp.float32), pltpu.SemaphoreType.DMA((2,))],
         compiler_params=pltpu.CompilerParams(vmem_limit_bytes=VMEM_BYTES),
         name='add_rows',
-    )(keys, starts, counts, base, *rows)
+    )(ids, starts, counts, *rows)
 
 
 def rope_tables(positions, head_dim):
@@ -573,23 +726,25 @@
         order = jnp.arange(seq, dtype=jnp.int32)
         keys = ids * seq + order
         rank = jnp.sum((keys[None, :] < keys[:, None]).astype(jnp.int32), axis=1)
-        sorted_keys = jnp.sum(jnp.where(rank[None, :] == order[:, None], keys[None, :], 0), axis=1)
-        all_keys = gather_ids(jnp.concatenate([ids, sorted_keys]).reshape(2 * seq // LANES, LANES)).reshape(N_DEV, 2, seq)
+        sorted_ids = jnp.sum(jnp.where(rank[None, :] == order[:, None], ids[None, :], 0), axis=1)
+        all_keys = gather_ids(jnp.concatenate([ids, sorted_ids]).reshape(2 * seq // LANES, LANES)).reshape(N_DEV, 2, seq)
         all_ids = all_keys[:, 0]
-        all_keys = all_keys[:, 1]
+        sorted_all = all_keys[:, 1]
         chip_ids = (all_ids - me // NC * (NC * rows_local)).reshape(-1)
         width_p = SUBL * LANES
         table_rows = jnp.pad(table_shard, ((0, 0), (0, width_p - dim))).reshape(rows_local, SUBL, LANES)
         x_emb = fetch_rows(chip_ids, table_rows, seq).reshape(seq, width_p)[:, :dim].astype(jnp.float32)
-        low = me * (rows_local * seq)
-        my_starts = jnp.sum((all_keys < low).astype(jnp.int32), axis=1)
-        my_counts = jnp.sum((all_keys < low + rows_local * seq).astype(jnp.int32), axis=1) - my_starts
+        low = me * rows_local
+        my_starts = jnp.sum((sorted_all < low).astype(jnp.int32), axis=1)
+        my_counts = jnp.sum((sorted_all < low + rows_local).astype(jnp.int32), axis=1) - my_starts
+        local_ids = jnp.clip(sorted_all - low, 0, rows_local - 1).reshape(-1)
 
         norm_pad = ((0, 0), (0, LANES - part))
         gains = jnp.concatenate([jnp.pad(attn_norm_s[None], norm_pad), jnp.pad(mlp_norm_s[None], norm_pad), jnp.zeros((14, LANES), attn_norm_s.dtype)], axis=0)
         w_qkv = jnp.concatenate([w_query, w_key, w_value], axis=1)
-        blocks = [gains, pad_rows(w_qkv, part_p), pad_rows(w_out, part_p), pad_rows(w_gate, part_p), pad_rows(w_up, part_p), w_down]
-        gains_all, w_qkv_p, w_out_p, w_gate_p, w_up_p, w_down_f = gather_blocks(blocks, 1, 'gather_weights')
+        blocks = [gains, pad_rows(w_qkv, part_p), pad_rows(w_out, part_p)]
+        gains_all, w_qkv_p, w_out_p = gather_blocks(blocks, 0, 1, 'gather_weights')
+        w_gate_p, w_up_p, w_down_f = (lax.all_gather(w, AXIS_NAME, tiled=True) for w in (pad_rows(w_gate, part_p), pad_rows(w_up, part_p), w_down))
         attn_norm = gains_all[:, 0, :part].reshape(dim)
         mlp_norm = gains_all[:, 1, :part].reshape(dim)
         w_qkv_p, w_out_p, w_gate_p, w_up_p, w_down_f = (w.reshape(-1, w.shape[-1]) for w in (w_qkv_p, w_out_p, w_gate_p, w_up_p, w_down_f))
@@ -652,17 +807,18 @@
         grad_qkv = jnp.concatenate([grad_q_raw, grad_k_raw, grad_v_raw], axis=1)
         grad_attn_in = narrow(dot_nt(grad_qkv, w_qkv_p))
         grad_x_emb = grad_hidden + norm_bwd(grad_attn_in, normed1, norm1_inv, attn_norm)
-        dx_rows = jnp.pad(grad_x_emb, ((0, 0), (0, width_p - dim))).reshape(DX_CHUNKS, seq * SUBL // DX_CHUNKS, LANES)
-        dx_all = gather_blocks([dx_rows[h] for h in range(DX_CHUNKS)], 4, 'gather_dx')
+        dx_rows = pack_rows(rank, grad_x_emb)
+        dx_all = gather_blocks(dx_rows, 1, 4, 'gather_dx')
 
         grad_attn_norm = jnp.sum(grad_attn_in * normed1, axis=0)
         grad_w_qkv = dot_t(attn_in, grad_qkv)
         small = jnp.stack([jnp.pad(grad_attn_norm.reshape(N_DEV, part), norm_pad), jnp.pad(grad_mlp_norm.reshape(N_DEV, part), norm_pad),
                            jnp.broadcast_to(jnp.concatenate([grad_q_norm, grad_k_norm])[None], (N_DEV, 2 * head_dim))], axis=1)
         small = jnp.pad(small, ((0, 0), (0, SUBL - 3), (0, 0)))
-        parts = [small] + [g.reshape(N_DEV, -1, g.shape[-1]) for g in (grad_w_qkv, grad_w_out, grad_w_gate, grad_w_up, grad_w_down)]
-        small_s, qkv_s, out_s, gate_s, up_s, down_s = scatter_grads(parts)
-        d_table = add_rows(all_keys.reshape(-1), my_starts, my_counts, (me * rows_local).reshape(1), dx_all, rows_local, dim)
+        parts = [small] + [g.reshape(N_DEV, -1, g.shape[-1]) for g in (grad_w_qkv, grad_w_out, grad_w_gate, grad_w_up,)]
+        small_s, qkv_s, out_s, gate_s, up_s = scatter_grads(parts)
+        down_s, = (lax.psum_scatter(g, AXIS_NAME, scatter_dimension=0, tiled=True) for g in (grad_w_down,))
+        d_table = add_rows(local_ids, my_starts, my_counts, dx_all, rows_local, dim)
         return (layer_out[None], d_table, small_s[0, :part], qkv_s[:part, :n_q], qkv_s[:part, n_q:n_q + n_kv], qkv_s[:part, n_q + n_kv:],
                 small_s[2, :head_dim], small_s[2, head_dim:], out_s[:part], small_s[1, :part], gate_s[:part], up_s[:part], down_s)
 

time: 1120 us -> 1010 us (0.902)
  the two profiles are of different devices: /device:TPU:23 before, /device:TPU:0 now
where the time goes in v2:
time: 1010 us
  Pallas kernels  710 us (70%)
  matrix products  168 us (17%)
  local copies, waits for them, and re-layouts  76.8 us (8%)
  other arithmetic  34.5 us (3%)
  between operations  15.1 us (1%)
    pallas_call x2, Pallas kernels, gather_blocks(): pl.pallas_call(functools.partial(blocks_kernel, n_a, n_b, stacked), out_s...  344 us
    pallas_call x1, Pallas kernels, fetch_rows(): pl.pallas_call(rows_kernel, out_shape=jax.ShapeDtypeStruct((seq,) + row,...  174 us
    pallas_call x1, Pallas kernels, scatter_grads(): pl.pallas_call(functools.partial(grads_kernel, n_arr), out_shape=tuple((j...  138 us
    pallas_call x1, Pallas kernels, add_rows(): pl.pallas_call(add_kernel, out_shape=jax.ShapeDtypeStruct((n_out, width),...  38.1 us
    unnamed x135, local copies, waits for them, and re-layouts  36.8 us
    dot_general x8, matrix products, dot_f32(): return jnp.dot(lhs, rhs, preferred_element_type=jnp.float32)  32.1 us
    dot_general x5, matrix products, dot_nt(): lax.dot_general(lhs, rhs, (((1,), (1,)), ((), ())), preferred_element_typ...  30.7 us
    dot_general x5, matrix products, dot_t(): lax.dot_general(lhs, rhs, (((0,), (0,)), ((), ())), preferred_element_typ...  25.5 us
  transfers between devices with their start and end apart: 4, of which 0 were waited for; matrix products, arithmetic and copies ran while one was open for 23% of the time, Pallas kernels for 71%

profile of v2, /device:TPU:0, one launch (start us, length us, event | category | flops | bytes accessed | tf_op | source)
XLA Modules:
  0.0 1005.0 jit_solution(7172913124170525401)
XLA Ops:
  21.1 12.3 %gather_ids.1 = s32[32,8,128]{2,1,0:T(8,128)} custom-call(s32[8,128]{1,0:T(8,128)} %pad_add_fusion.src), custom_call_target="tpu_custom_call" | custom-call | tf_op jit(solution)/shard_map/gather_ids/pallas_call | solution.py:78
  44.4 174.0 %fetch_rows.1 = bf16[512,8,128]{2,1,0:T(8,128)(2,1)S(1)} custom-call(s32[16384]{0:T(1024)S(1)} %bitcast.191, bf16[1536,8,128]{2,1,0:T(8,128)(2,1)S(1)} %copy.87.table), custom_call_target="tpu_custom_call" | custom-call | tf_op jit(solution)/shard_map/fetch_rows/pallas_call | solution.py:487
  218.8 59.7 %gather_weights.1 = (bf16[32,16,128]{2,1,0:T(8,128)(2,1)S(1)}, bf16[32,32,1600]{2,1,0:T(8,128)(2,1)S(1)}, bf16[32,32,960]{2,1,0:T(8,128)(2,1)S(1)}) custom-call(bf16[16,128]{1,0:T(8,128)(2,1)S(1)} %fusion.105.refs_0_, bf16[32,1600]{1,0:T(8,128)(2,1)S(1)} %pad.40.refs_1_, bf16[32,960]{1,0:T(8,128)(2,1)S(1)} %pad.41.refs_2_), custom_call_target="tpu_custom_call" | custom-call | tf_op jit(solution)/shard_map/gather_weights/pallas_call | solution.py:259
  291.6 12.9 %fusion.122 = (f32[5,3,512]{2,1,0:T(4,128)}, f32[5,3,512,512]{2,3,1,0:T(8,128)}) fusion(pred[512,512]{0,1:T(8,128)(4,1)} %iota_compare_fusion.13, bf16[512,5,3,32]{0,3,2,1:T(8,128)(2,1)} %get-tuple-element.90, bf16[512,5,3,32]{0,3,2,1:T(8,128)(2,1)} %get-tuple-element.89, bf16[512,5,32]{0,2,1:T(8,128)(2,1)} %get-tuple-element.102, ...), kind=kOutput, calls=%fused_computation.198 | convolution fusion | flops 521667072 | bytes 17332224 | tf_op jit(solution)/shard_map/sub | solution.py:672
  304.5 7.4 fusion.59
  318.3 8.0 fusion.124
  326.3 8.1 fusion.123
  334.4 10.9 %multiply_convert_fusion = (bf16[512,2560]{1,0:T(8,128)(2,1)}, bf16[512,2560]{1,0:T(8,128)(2,1)}, bf16[512,2560]{1,0:T(8,128)(2,1)S(1)}) fusion(f32[512,2560]{1,0:T(8,128)} %fusion.123, f32[512,2560]{1,0:T(8,128)} %fusion.124, bf16[2560,960]{1,0:T(8,128)(2,1)} %all-gather.8.cloned.1.call-done, bf16[1,512,960]{1,2,0:T(8,128)(2,1)S(1)} %copy-done.25), kind=kOutput, calls=%fused_computation.17 | convolution fusion | flops 2537553920 | bytes 24248320 | tf_op jit(solution)/shard_map/dot_general | solution.py:698
  346.8 5.8 fusion.77
  361.3 7.2 fusion.63
  370.7 5.8 fusion.125
  376.6 6.7 convolution_add_fusion
  404.6 7.8 fusion.126
  412.4 21.4 %fusion.64 = f32[512,5,64]{0,2,1:T(8,128)S(1)} fusion(f32[5,512,512,3]{2,1,3,0:T(8,128)} %fusion.126, bf16[512,5,3,32]{0,3,2,1:T(8,128)(2,1)} %get-tuple-element.90, bf16[512,5,3,32]{0,3,2,1:T(8,128)(2,1)S(1)} %copy-done.29, f32[5,3,512,512]{2,3,1,0:T(8,128)} %get-tuple-element.117, f32[5,3,512]{2,1,0:T(4,128)S(1)} %copy-done.62), kind=kOutput, calls=%fused_computation.89 | convolution fusion | flops 532815872 | bytes 33126400 | tf_op jit(solution)/shard_map/grqk,qgrh->kgh/dot_general | solution.py:685
  436.3 21.9 %fusion.55 = f32[512,5,3,64]{0,3,2,1:T(8,128)S(1)} fusion(f32[5,512,512,3]{2,1,3,0:T(8,128)} %fusion.126, bf16[512,5,32]{0,2,1:T(8,128)(2,1)} %get-tuple-element.102, bf16[512,5,32]{0,2,1:T(8,128)(2,1)} %get-tuple-element.101, f32[5,3,512,512]{2,3,1,0:T(8,128)} %get-tuple-element.117, f32[5,3,512]{2,1,0:T(4,128)S(1)} %copy-done.62), kind=kOutput, calls=%fused_computation.80 | convolution fusion | flops 531505152 | bytes 33781760 | tf_op jit(solution)/shard_map/grqk,kgh->qgrh/dot_general | solution.py:684
  462.9 8.4 fusion.68
  500.6 5.6 fusion.128
  506.2 5.8 fusion.127
  512.0 138.1 %scatter_grads.1 = (f32[8,128]{1,0:T(8,128)}, f32[32,1600]{1,0:T(8,128)}, f32[32,960]{1,0:T(8,128)}, f32[32,2560]{1,0:T(8,128)}, f32[32,2560]{1,0:T(8,128)}) custom-call(f32[32,8,128]{2,1,0:T(8,128)} %select_maximum_fusion.refs_0_, f32[32,32,1600]{2,1,0:T(8,128)} %bitcast.212, f32[32,32,960]{2,1,0:T(8,128)} %bitcast.198, f32[32,32,2560]{2,1,0:T(8,128)} %bitcast.207, ...), custom_call_target="tpu_custom_call" | custom-call | tf_op jit(solution)/shard_map/scatter_grads/pallas_call | solution.py:381
  653.3 283.8 %gather_dx.1 = (f32[32,1024,128]{2,1,0:T(8,128)S(1)}, f32[32,1024,128]{2,1,0:T(8,128)S(1)}, f32[32,1024,128]{2,1,0:T(8,128)}, f32[32,1024,128]{2,1,0:T(8,128)}) custom-call(f32[4,1024,128]{2,1,0:T(8,128)S(1)} %copy-done.3), custom_call_target="tpu_custom_call" | custom-call | tf_op jit(solution)/shard_map/gather_dx/pallas_call | solution.py:259
  937.1 5.7 copy-done
  942.8 5.7 copy-done.1
  948.5 38.1 %add_rows.1 = f32[1536,960]{1,0:T(8,128)} custom-call(s32[16384]{0:T(1024)} %bitcast.220, s32[32]{0:T(128)} %get-tuple-element.81.starts, s32[32]{0:T(128)} %sub.93.counts, f32[32,1024,128]{2,1,0:T(8,128)} %copy-done, f32[32,1024,128]{2,1,0:T(8,128)} %copy-done.1, f32[32,1024,128]{2,1,0:T(8,128)} %get-tuple-element.30.refs_2_, ...), custom_call_target="tpu_custom_call" | custom-call | tf_op jit(solution)/shard_map/add_rows/pallas_call | solution.py:628
  986.7 6.5 copy.74
  (235 shorter events, 122.3 us)
Async XLA Ops:
  7.2 311.1 %all-gather.6.cloned.1.call-start = ((), (), s32[]{:S(2)}) async-start(), calls=%async_computation.2 | async-start | bytes 5406720 | tf_op jit(solution)/shard_map/all_gather | solution.py:747
  8.8 317.4 %all-gather.4.cloned.1.call-start = ((), (), s32[]{:S(2)}) async-start(), calls=%async_computation.1 | async-start | bytes 5406720 | tf_op jit(solution)/shard_map/all_gather | solution.py:747
  10.5 323.9 %all-gather.8.cloned.1.call-start = ((), (), s32[]{:S(2)}) async-start(), calls=%async_computation.3 | async-start | bytes 5406720 | tf_op jit(solution)/shard_map/all_gather | solution.py:747
  11.3 984.6 %reduce-scatter.2.cloned.1.call-start = ((), (), s32[]{:S(2)}) async-start(), calls=%async_computation.4 | async-start | bytes 10813440 | tf_op jit(solution)/shard_map/reduce_scatter | solution.py:820
  44.4 174.4 %copy-start.51 = (bf16[30]{0:T(256)(128)(2,1)S(1)}, bf16[30]{0:T(256)(128)(2,1)}, u32[]{:S(2)}) copy-start(bf16[30]{0:T(256)(128)(2,1)} %param.25) | copy-start | bytes 184
  44.4 174.4 %copy-start.52 = (bf16[30]{0:T(256)(128)(2,1)S(1)}, bf16[30]{0:T(256)(128)(2,1)}, u32[]{:S(2)}) copy-start(bf16[30]{0:T(256)(128)(2,1)} %param.18) | copy-start | bytes 184
  218.6 94.7 %copy-start.13 = (bf16[64,8,8,128]{3,1,2,0:T(8,128)(2,1)}, bf16[64,8,8,128]{3,1,2,0:T(8,128)(2,1)S(1)}, u32[]{:S(2)}) copy-start(bf16[64,8,8,128]{3,1,2,0:T(8,128)(2,1)S(1)} %copy.90) | copy-start | bytes 3145732
  304.5 7.4 copy-start.44
  326.3 8.1 copy-start.25
  352.6 8.7 copy-start.20
  370.7 5.8 copy-start.58
  404.6 7.8 copy-start.29
  404.6 7.8 copy-start.62
  412.4 21.4 %copy-start.28 = (f32[512,32]{0,1:T(8,128)S(1)}, f32[512,32]{0,1:T(8,128)}, u32[]{:S(2)}) copy-start(f32[512,32]{0,1:T(8,128)} %get-tuple-element.113) | copy-start | bytes 196612
  412.4 21.5 %copy-start.16 = (f32[512,320]{0,1:T(8,128)S(1)}, f32[512,320]{0,1:T(8,128)}, u32[]{:S(2)}) copy-start(f32[512,320]{0,1:T(8,128)} %copy-done.15) | copy-start | bytes 1966084
  412.4 21.5 %copy-start.46 = (f32[64]{0:T(128)S(1)}, f32[64]{0:T(128)}, u32[]{:S(2)}) copy-start(f32[64]{0:T(128)} %convert_element_type.179) | copy-start | bytes 772
  462.9 8.4 copy-start.23
  462.9 9.1 copy-start.8
  486.4 5.9 copy-start.22
  937.1 5.7 copy-start
  986.6 6.5 copy-start.49
  986.6 9.2 copy-start.32
  986.7 9.9 copy-start.31
  986.7 10.6 %copy-start.30 = (f32[32,2560]{1,0:T(8,128)S(1)}, f32[32,2560]{1,0:T(8,128)}, u32[]{:S(2)}) copy-start(f32[32,2560]{1,0:T(8,128)} %get-tuple-element.36) | copy-start | bytes 983044
  (44 other events, 108.4 us)
Sparse Core Ops, SparseCore 0:
  10.8 74.5 all-gather.5
  88.9 112.2 all-gather.3
  204.0 79.2 all-gather.7
  352.8 149.0 reduce-scatter.1

commit v3 on v2

--- a/solution.py
+++ b/solution.py
@@ -86,16 +86,22 @@
     )(block)
 
 
-def blocks_kernel(n_a, n_b, stacked, *refs):
+def blocks_kernel(n_a, n_b, cuts, *refs):
     n_arr = n_a + n_b
+    stacked = cuts is not None
     if stacked:
-        ins = [refs[0].at[a] for a in range(n_arr)]
+        ins = [refs[0].at[pl.ds(first_row, n_rows)] for first_row, n_rows in cuts]
         refs = refs[1:]
     else:
         ins = refs[:n_arr]
         refs = refs[n_arr:]
-    outs = refs[:n_arr]
-    loc_sem, az_send, az_recv, ar_send, ar_recv, ap_send, ap_recv, bz_send, bz_recv, br_send, br_recv, bp_send, bp_recv = refs[n_arr:]
+    if stacked:
+        outs = [refs[0].at[:, pl.ds(first_row, n_rows)] for first_row, n_rows in cuts]
+        refs = refs[1:]
+    else:
+        outs = refs[:n_arr]
+        refs = refs[n_arr:]
+    loc_sem, az_send, az_recv, ar_send, ar_recv, ap_send, ap_recv, bz_send, bz_recv, br_send, br_recv, bp_send, bp_recv = refs
     me, z, q, c = my_coords()
     step_dir = 1 - 2 * c
     nxt = dev_id(z, wrap4(q + step_dir), c)
@@ -248,24 +254,27 @@
                     spread(a, t, s, settle)
 
 
-def gather_blocks(blocks, n_b, collective_id, name):
-    stacked = not isinstance(blocks, list)
-    n_arr = blocks.shape[0] if stacked else len(blocks)
+def gather_blocks(blocks, n_b, collective_id, name, cuts=None):
+    stacked = cuts is not None
+    n_arr = len(cuts) if stacked else len(blocks)
     n_a = n_arr - n_b
     n_b1 = max(n_b, 1)
-    out_shape = tuple(jax.ShapeDtypeStruct((N_DEV,) + blocks[a].shape, blocks[a].dtype) for a in range(n_arr))
+    out_shape = tuple(jax.ShapeDtypeStruct((N_DEV,) + b.shape, b.dtype) for b in ([blocks] if stacked else blocks))
     dma = pltpu.SemaphoreType.DMA
     operands = [blocks] if stacked else blocks
     return pl.pallas_call(
-        functools.partial(blocks_kernel, n_a, n_b, stacked),
+        functools.partial(blocks_kernel, n_a, n_b, cuts),
         out_shape=out_shape,
         in_specs=[pl.BlockSpec(memory_space=pltpu.VMEM)] * len(operands),
-        out_specs=tuple(pl.BlockSpec(memory_space=pltpu.HBM) for _ in range(n_arr)),
+        out_specs=tuple(pl.BlockSpec(memory_space=pltpu.HBM) for _ in out_shape),
         scratch_shapes=[dma((n_arr,)), dma((n_a, 2, 4)), dma((n_a, 4)), dma((n_a, 3, 4)), dma((n_a, 3, 4)), dma((n_a, 4, 4)), dma((n_a, 4, 4)),
                         dma((n_b1, 4, 2, 4)), dma((n_b1, 4, 4)), dma((n_b1, 3)), dma((n_b1, 3)), dma((n_b1, 4, 4)), dma((n_b1, 4, 4))],
         compiler_params=pltpu.CompilerParams(collective_id=collective_id, has_side_effects=True, vmem_limit_bytes=8 * 1024 * 1024),
         name=name,
     )(*operands)
+
+
+N_GROUPS = 16
 
 
 def grads_kernel(n_arr, *refs):
@@ -498,11 +507,11 @@
 
 N_ACC = 4
 DX_CHUNKS = 4
+DX_CUTS = (144, 136, 136, 96)
 
 
 def pack_kernel(rank, dx, out, tmp):
     seq, width = dx.shape
-    part = seq // DX_CHUNKS
 
     @pl.loop(0, seq // SUBL)
     def _(r):
@@ -518,9 +527,8 @@
     def _(r):
         for u in range(SUBL):
             i = r * SUBL + u
-            place = rank[i]
-            row = pl.multiple_of(lax.rem(place, part) * SUBL, SUBL)
-            out[lax.div(place, part), pl.ds(row, SUBL), :] = tmp[pl.ds(pl.multiple_of(i * SUBL, SUBL), SUBL), :]
+            row = pl.multiple_of(rank[i] * SUBL, SUBL)
+            out[pl.ds(row, SUBL), :] = tmp[pl.ds(pl.multiple_of(i * SUBL, SUBL), SUBL), :]
 
 
 def pack_rows(rank, dx):
@@ -528,7 +536,7 @@
     vmem = pl.BlockSpec(memory_space=pltpu.VMEM)
     return pl.pallas_call(
         pack_kernel,
-        out_shape=jax.ShapeDtypeStruct((DX_CHUNKS, seq * SUBL // DX_CHUNKS, LANES), dx.dtype),
+        out_shape=jax.ShapeDtypeStruct((seq * SUBL, LANES), dx.dtype),
         in_specs=[pl.BlockSpec(memory_space=pltpu.SMEM), vmem],
         out_specs=vmem,
         scratch_shapes=[pltpu.VMEM((seq * SUBL, LANES), dx.dtype)],
@@ -540,18 +548,16 @@
 OUT_ROWS = 128
 
 
-def add_kernel(ids, starts, counts, *refs):
-    rows = refs[:DX_CHUNKS]
-    out = refs[DX_CHUNKS]
-    accs = refs[DX_CHUNKS + 1:DX_CHUNKS + 1 + N_ACC]
-    buf, sem, stage, stage_sem = refs[DX_CHUNKS + 1 + N_ACC:]
-    n_out, width = out.shape
+def add_kernel(ids, starts, counts, rows, out, *refs):
+    accs = refs[:N_ACC]
+    buf, sem, stage, stage_sem = refs[N_ACC:]
+    width, n_out = out.shape
     seq = buf.shape[1] // SUBL
     part = seq // DX_CHUNKS
 
     def load(i, h):
         slot = lax.rem(i, 3)
-        return pltpu.make_async_copy(rows[h].at[i], buf.at[slot, pl.ds(h * part * SUBL, part * SUBL)], sem.at[slot, h])
+        return pltpu.make_async_copy(rows.at[i, pl.ds(h * part * SUBL, part * SUBL)], buf.at[slot, pl.ds(h * part * SUBL, part * SUBL)], sem.at[slot, h])
 
     def each_load(i, act):
         low, high = starts[i], starts[i] + counts[i]
@@ -599,7 +605,7 @@
 
     def store(m):
         here = pl.ds(pl.multiple_of(m * OUT_ROWS, OUT_ROWS), OUT_ROWS)
-        return pltpu.make_async_copy(stage.at[lax.rem(m, 2)], out.at[here], stage_sem.at[lax.rem(m, 2)])
+        return pltpu.make_async_copy(stage.at[lax.rem(m, 2)], out.at[:, here], stage_sem.at[lax.rem(m, 2)])
     n_store = n_out // OUT_ROWS
 
     @pl.loop(0, n_store)
@@ -607,16 +613,17 @@
         @pl.when(m >= 2)
         def _():
             store(m - 2).wait()
-
-        @pl.loop(0, OUT_ROWS // SUBL)
-        def _(r):
-            for j in range(SUBL):
-                lanes = min(LANES, width - j * LANES)
+        for j in range(SUBL):
+            lanes = min(LANES, width - j * LANES)
+            pieces = []
+            for r in range(OUT_ROWS // SUBL):
                 here = pl.ds(m * (OUT_ROWS * SUBL) + r * (SUBL * SUBL) + j, SUBL, stride=SUBL)
                 value = accs[0][here, :]
                 for acc in accs[1:]:
                     value = value + acc[here, :]
-                stage[lax.rem(m, 2), pl.ds(pl.multiple_of(r * SUBL, SUBL), SUBL), pl.ds(j * LANES, lanes)] = value[:, :lanes]
+                pieces.append(value)
+            flipped = jnp.concatenate(pieces, axis=0).T
+            stage[lax.rem(m, 2), pl.ds(j * LANES, lanes), :] = flipped[:lanes]
         store(m).start()
     for m in (n_store - 2, n_store - 1):
         store(m).wait()
@@ -624,18 +631,18 @@
 
 def add_rows(ids, starts, counts, rows, n_out, width):
     smem = pl.BlockSpec(memory_space=pltpu.SMEM)
-    seq_rows = DX_CHUNKS * rows[0].shape[1]
+    seq_rows = rows.shape[1]
     return pl.pallas_call(
         add_kernel,
-        out_shape=jax.ShapeDtypeStruct((n_out, width), jnp.float32),
-        in_specs=[smem] * 3 + [pl.BlockSpec(memory_space=pltpu.HBM)] * DX_CHUNKS,
+        out_shape=jax.ShapeDtypeStruct((width, n_out), jnp.float32),
+        in_specs=[smem] * 3 + [pl.BlockSpec(memory_space=pltpu.HBM)],
         out_specs=pl.BlockSpec(memory_space=pltpu.HBM),
         scratch_shapes=[pltpu.VMEM((n_out * SUBL, LANES), jnp.float32)] * N_ACC + [
             pltpu.VMEM((3, seq_rows, LANES), jnp.float32), pltpu.SemaphoreType.DMA((3, DX_CHUNKS)),
-            pltpu.VMEM((2, OUT_ROWS, width), jnp.float32), pltpu.SemaphoreType.DMA((2,))],
+            pltpu.VMEM((2, width, OUT_ROWS), jnp.float32), pltpu.SemaphoreType.DMA((2,))],
         compiler_params=pltpu.CompilerParams(vmem_limit_bytes=VMEM_BYTES),
         name='add_rows',
-    )(ids, starts, counts, *rows)
+    )(ids, starts, counts, rows).T
 
 
 def rope_tables(positions, head_dim):
@@ -808,7 +815,8 @@
         grad_attn_in = narrow(dot_nt(grad_qkv, w_qkv_p))
         grad_x_emb = grad_hidden + norm_bwd(grad_attn_in, normed1, norm1_inv, attn_norm)
         dx_rows = pack_rows(rank, grad_x_emb)
-        dx_all = gather_blocks(dx_rows, 1, 4, 'gather_dx')
+        cuts = [(SUBL * sum(DX_CUTS[:h]), SUBL * DX_CUTS[h]) for h in range(len(DX_CUTS))]
+        dx_all, = gather_blocks(dx_rows, 1, 4, 'gather_dx', cuts)
 
         grad_attn_norm = jnp.sum(grad_attn_in * normed1, axis=0)
         grad_w_qkv = dot_t(attn_in, grad_qkv)

time: 1010 us -> 986 us (0.976)
  local copies, waits for them, and re-layouts: 76.8 us -> 58.8 us
    unnamed x135 -> x130, local copies, waits for them, and re-layouts: 36.8 us -> 18.9 us
  transfers between devices with their start and end apart: 4 -> 4, of which waited for: 0 -> 0; matrix products, arithmetic and copies ran while one was open for 23% -> 23% of each run, Pallas kernels for 71% -> 72%
where the time goes in v3:
time: 986 us; the launch traced here: 980 us
  Pallas kernels  702 us (71%)
  matrix products  168 us (17%)
  local copies, waits for them, and re-layouts  58.8 us (6%)
  other arithmetic  34.5 us (3%)
  between operations  15.1 us (2%)
    pallas_call x2, Pallas kernels, gather_blocks(): pl.pallas_call(functools.partial(blocks_kernel, n_a, n_b, cuts), out_shap...  338 us
    pallas_call x1, Pallas kernels, fetch_rows(): pl.pallas_call(rows_kernel, out_shape=jax.ShapeDtypeStruct((seq,) + row,...  174 us
    pallas_call x1, Pallas kernels, scatter_grads(): pl.pallas_call(functools.partial(grads_kernel, n_arr), out_shape=tuple((j...  138 us
    pallas_call x1, Pallas kernels, add_rows(): pl.pallas_call(add_kernel, out_shape=jax.ShapeDtypeStruct((width, n_out),...  37.8 us
    dot_general x8, matrix products, dot_f32(): return jnp.dot(lhs, rhs, preferred_element_type=jnp.float32)  32.1 us
    dot_general x5, matrix products, dot_nt(): lax.dot_general(lhs, rhs, (((1,), (1,)), ((), ())), preferred_element_typ...  30.8 us
    dot_general x5, matrix products, dot_t(): lax.dot_general(lhs, rhs, (((0,), (0,)), ((), ())), preferred_element_typ...  25.6 us
    dot_general x1, matrix products, attn_bwd(): jnp.einsum('grqk,kgh->qgrh', scores_b, k_rot, preferred_element_type=jnp....  21.9 us
  transfers between devices with their start and end apart: 4, of which 0 were waited for; matrix products, arithmetic and copies ran while one was open for 23% of the time, Pallas kernels for 72%

profile of v3, /device:TPU:0, one launch (start us, length us, event | category | flops | bytes accessed | tf_op | source)
XLA Modules:
  0.0 979.7 jit_solution(7191820783773164782)
XLA Ops:
  21.1 12.3 %gather_ids.1 = s32[32,8,128]{2,1,0:T(8,128)} custom-call(s32[8,128]{1,0:T(8,128)} %pad_add_fusion.src), custom_call_target="tpu_custom_call" | custom-call | tf_op jit(solution)/shard_map/gather_ids/pallas_call | solution.py:78
  44.4 174.0 %fetch_rows.1 = bf16[512,8,128]{2,1,0:T(8,128)(2,1)S(1)} custom-call(s32[16384]{0:T(1024)S(1)} %bitcast.192, bf16[1536,8,128]{2,1,0:T(8,128)(2,1)S(1)} %copy.84.table), custom_call_target="tpu_custom_call" | custom-call | tf_op jit(solution)/shard_map/fetch_rows/pallas_call | solution.py:496
  218.9 59.7 %gather_weights.1 = (bf16[32,16,128]{2,1,0:T(8,128)(2,1)S(1)}, bf16[32,32,1600]{2,1,0:T(8,128)(2,1)S(1)}, bf16[32,32,960]{2,1,0:T(8,128)(2,1)S(1)}) custom-call(bf16[16,128]{1,0:T(8,128)(2,1)S(1)} %fusion.105.refs_0_, bf16[32,1600]{1,0:T(8,128)(2,1)S(1)} %pad.40.refs_1_, bf16[32,960]{1,0:T(8,128)(2,1)S(1)} %pad.41.refs_2_), custom_call_target="tpu_custom_call" | custom-call | tf_op jit(solution)/shard_map/gather_weights/pallas_call | solution.py:265
  291.5 13.0 %fusion.122 = (f32[5,3,512]{2,1,0:T(4,128)}, f32[5,3,512,512]{2,3,1,0:T(8,128)}) fusion(pred[512,512]{0,1:T(8,128)(4,1)} %iota_compare_fusion.13, bf16[512,5,3,32]{0,3,2,1:T(8,128)(2,1)} %get-tuple-element.82, bf16[512,5,3,32]{0,3,2,1:T(8,128)(2,1)} %get-tuple-element.81, bf16[512,5,32]{0,2,1:T(8,128)(2,1)} %get-tuple-element.94, ...), kind=kOutput, calls=%fused_computation.198 | convolution fusion | flops 521667072 | bytes 17332224 | tf_op jit(solution)/shard_map/sub | solution.py:679
  304.4 7.4 fusion.59
  318.2 8.0 fusion.124
  326.2 8.1 fusion.123
  334.3 10.9 %multiply_convert_fusion = (bf16[512,2560]{1,0:T(8,128)(2,1)}, bf16[512,2560]{1,0:T(8,128)(2,1)}, bf16[512,2560]{1,0:T(8,128)(2,1)S(1)}) fusion(f32[512,2560]{1,0:T(8,128)} %fusion.123, f32[512,2560]{1,0:T(8,128)} %fusion.124, bf16[2560,960]{1,0:T(8,128)(2,1)} %all-gather.8.cloned.1.call-done, bf16[1,512,960]{1,2,0:T(8,128)(2,1)S(1)} %copy-done.23), kind=kOutput, calls=%fused_computation.17 | convolution fusion | flops 2537553920 | bytes 24248320 | tf_op jit(solution)/shard_map/dot_general | solution.py:705
  346.7 5.8 fusion.77
  361.3 7.1 fusion.63
  370.7 5.8 fusion.125
  376.5 6.7 convolution_add_fusion
  396.8 3.8 fusion.42
  400.6 3.9 fusion.62
  404.6 7.8 fusion.126
  412.4 21.4 %fusion.64 = f32[512,5,64]{0,2,1:T(8,128)S(1)} fusion(f32[5,512,512,3]{2,1,3,0:T(8,128)} %fusion.126, bf16[512,5,3,32]{0,3,2,1:T(8,128)(2,1)} %get-tuple-element.82, bf16[512,5,3,32]{0,3,2,1:T(8,128)(2,1)S(1)} %copy-done.27, f32[5,3,512,512]{2,3,1,0:T(8,128)} %get-tuple-element.109, f32[5,3,512]{2,1,0:T(4,128)S(1)} %copy-done.60), kind=kOutput, calls=%fused_computation.89 | convolution fusion | flops 532815872 | bytes 33126400 | tf_op jit(solution)/shard_map/grqk,qgrh->kgh/dot_general | solution.py:692
  436.3 21.9 %fusion.55 = f32[512,5,3,64]{0,3,2,1:T(8,128)S(1)} fusion(f32[5,512,512,3]{2,1,3,0:T(8,128)} %fusion.126, bf16[512,5,32]{0,2,1:T(8,128)(2,1)} %get-tuple-element.94, bf16[512,5,32]{0,2,1:T(8,128)(2,1)} %get-tuple-element.93, f32[5,3,512,512]{2,3,1,0:T(8,128)} %get-tuple-element.109, f32[5,3,512]{2,1,0:T(4,128)S(1)} %copy-done.60), kind=kOutput, calls=%fused_computation.80 | convolution fusion | flops 531505152 | bytes 33781760 | tf_op jit(solution)/shard_map/grqk,kgh->qgrh/dot_general | solution.py:691
  462.9 8.4 fusion.68
  494.1 5.0 fusion.81
  499.1 5.6 fusion.128
  504.7 5.8 fusion.127
  510.5 138.1 %scatter_grads.1 = (f32[8,128]{1,0:T(8,128)}, f32[32,1600]{1,0:T(8,128)}, f32[32,960]{1,0:T(8,128)}, f32[32,2560]{1,0:T(8,128)}, f32[32,2560]{1,0:T(8,128)}) custom-call(f32[32,8,128]{2,1,0:T(8,128)} %select_maximum_fusion.refs_0_, f32[32,32,1600]{2,1,0:T(8,128)} %bitcast.213, f32[32,32,960]{2,1,0:T(8,128)} %bitcast.199, f32[32,32,2560]{2,1,0:T(8,128)} %bitcast.208, ...), custom_call_target="tpu_custom_call" | custom-call | tf_op jit(solution)/shard_map/scatter_grads/pallas_call | solution.py:390
  651.8 278.2 %gather_dx.1.rows = f32[32,4096,128]{2,1,0:T(8,128)} custom-call(f32[4096,128]{1,0:T(8,128)S(1)} %copy-done.1), custom_call_target="tpu_custom_call" | custom-call | tf_op jit(solution)/shard_map/gather_dx/pallas_call | solution.py:265
  930.0 37.8 %add_rows.1 = f32[960,1536]{1,0:T(8,128)} custom-call(s32[16384]{0:T(1024)} %bitcast.222, s32[32]{0:T(128)} %get-tuple-element.73.starts, s32[32]{0:T(128)} %sub.93.counts, f32[32,4096,128]{2,1,0:T(8,128)} %gather_dx.1.rows), custom_call_target="tpu_custom_call" | custom-call | tf_op jit(solution)/shard_map/add_rows/pallas_call | solution.py:635
  (230 shorter events, 108.1 us)
Async XLA Ops:
  7.2 311.0 %all-gather.6.cloned.1.call-start = ((), (), s32[]{:S(2)}) async-start(), calls=%async_computation.2 | async-start | bytes 5406720 | tf_op jit(solution)/shard_map/all_gather | solution.py:754
  8.8 317.3 %all-gather.4.cloned.1.call-start = ((), (), s32[]{:S(2)}) async-start(), calls=%async_computation.1 | async-start | bytes 5406720 | tf_op jit(solution)/shard_map/all_gather | solution.py:754
  10.5 323.8 %all-gather.8.cloned.1.call-start = ((), (), s32[]{:S(2)}) async-start(), calls=%async_computation.3 | async-start | bytes 5406720 | tf_op jit(solution)/shard_map/all_gather | solution.py:754
  11.2 959.3 %reduce-scatter.2.cloned.1.call-start = ((), (), s32[]{:S(2)}) async-start(), calls=%async_computation.4 | async-start | bytes 10813440 | tf_op jit(solution)/shard_map/reduce_scatter | solution.py:828
  44.4 174.4 %copy-start.49 = (bf16[30]{0:T(256)(128)(2,1)S(1)}, bf16[30]{0:T(256)(128)(2,1)}, u32[]{:S(2)}) copy-start(bf16[30]{0:T(256)(128)(2,1)} %param.25) | copy-start | bytes 184
  44.4 174.4 %copy-start.50 = (bf16[30]{0:T(256)(128)(2,1)S(1)}, bf16[30]{0:T(256)(128)(2,1)}, u32[]{:S(2)}) copy-start(bf16[30]{0:T(256)(128)(2,1)} %param.18) | copy-start | bytes 184
  218.7 94.6 %copy-start.11 = (bf16[64,8,8,128]{3,1,2,0:T(8,128)(2,1)}, bf16[64,8,8,128]{3,1,2,0:T(8,128)(2,1)S(1)}, u32[]{:S(2)}) copy-start(bf16[64,8,8,128]{3,1,2,0:T(8,128)(2,1)S(1)} %copy.87) | copy-start | bytes 3145732
  304.4 7.4 copy-start.42
  326.2 8.1 copy-start.23
  352.6 8.7 copy-start.18
  370.7 5.8 copy-start.56
  404.5 7.8 copy-start.27
  404.5 7.8 copy-start.60
  412.3 21.4 %copy-start.26 = (f32[512,32]{0,1:T(8,128)S(1)}, f32[512,32]{0,1:T(8,128)}, u32[]{:S(2)}) copy-start(f32[512,32]{0,1:T(8,128)} %get-tuple-element.105) | copy-start | bytes 196612
  412.3 21.5 %copy-start.14 = (f32[512,320]{0,1:T(8,128)S(1)}, f32[512,320]{0,1:T(8,128)}, u32[]{:S(2)}) copy-start(f32[512,320]{0,1:T(8,128)} %copy-done.13) | copy-start | bytes 1966084
  412.3 21.5 %copy-start.44 = (f32[64]{0:T(128)S(1)}, f32[64]{0:T(128)}, u32[]{:S(2)}) copy-start(f32[64]{0:T(128)} %convert_element_type.179) | copy-start | bytes 772
  462.9 8.4 copy-start.21
  462.9 9.1 copy-start.6
  480.1 5.5 copy-start.9
  499.1 5.6 copy-start.55
  930.0 37.8 %copy-start.47 = (f32[8,128]{1,0:T(8,128)S(1)}, f32[8,128]{1,0:T(8,128)}, u32[]{:S(2)}) copy-start(f32[8,128]{1,0:T(8,128)} %get-tuple-element.24) | copy-start | bytes 12292
  930.0 40.6 %copy-start.30 = (f32[32,960]{1,0:T(8,128)S(1)}, f32[32,960]{1,0:T(8,128)}, u32[]{:S(2)}) copy-start(f32[32,960]{1,0:T(8,128)} %get-tuple-element.26) | copy-start | bytes 368644
  930.0 41.2 %copy-start.29 = (f32[32,2560]{1,0:T(8,128)S(1)}, f32[32,2560]{1,0:T(8,128)}, u32[]{:S(2)}) copy-start(f32[32,2560]{1,0:T(8,128)} %get-tuple-element.27) | copy-start | bytes 983044
  930.0 41.9 %copy-start.28 = (f32[32,2560]{1,0:T(8,128)S(1)}, f32[32,2560]{1,0:T(8,128)}, u32[]{:S(2)}) copy-start(f32[32,2560]{1,0:T(8,128)} %get-tuple-element.28) | copy-start | bytes 983044
  (42 other events, 94.2 us)
Sparse Core Ops, SparseCore 0:
  10.8 74.5 all-gather.5
  88.9 112.2 all-gather.3
  204.0 79.2 all-gather.7
  352.7 148.9 reduce-scatter.1
